TPU v7x, 16 devices: a 4x2x1 block of a 4x4x8 slice. The times are simulated.
16 devices in a mesh: task: 2 (over y, z), row: 8 (over x, core).
Axes of the slice: x: 4, y: 2, z: 1, core: 2. Of those that a mesh axis runs over, the one named last changes fastest.
The devices are a block of a 4x4x8 slice.
Arguments:
- points: bfloat16 [32768, 768], P(('task', 'row')), parts along dimension 0
- vectors: bfloat16 [32768, 64], P(('task', 'row')), parts along dimension 0
- length_scale: float32 [2], P('task'), parts along dimension 0
- out_scale: float32 [2], P('task'), parts along dimension 0
Outputs:
- output: float32 [32768, 64], P(('task', 'row')), parts along dimension 0
There are 2 independent parts. A program takes and returns all parts, laid end to end along the dimension named above; each array names one.
All inputs are finite; a program needn't handle non-finite values.
Results may differ from a plain program's by a relative error of at most 0.001.
Values are sent between devices in bfloat16 or wider.
A program may use at most 768 MiB of HBM per device.

v0:
```python
import jax
import jax.numpy as jnp
from jax import lax
from jax.sharding import PartitionSpec as P


def solution(mesh):
    n_row = mesh.shape["row"]
    shift_pairs = [(source_idx, (source_idx + 1) % n_row) for source_idx in range(n_row)]

    def kernel_product(x_rows, norm_rows, x_cols, norm_cols, v_cols, length_scale, out_scale):
        gram_mat = jnp.einsum("if,jf->ij", x_rows, x_cols, preferred_element_type=jnp.float32)
        sq_dist = jnp.maximum(norm_rows[:, None] + norm_cols[None, :] - 2.0 * gram_mat, 0.0)
        kern_tile = (out_scale * jnp.exp(-sq_dist / (2.0 * length_scale * length_scale))).astype(jnp.bfloat16)
        return jnp.dot(kern_tile, v_cols, preferred_element_type=jnp.float32)

    def kernel_pass(x_loc, norm_loc, v_loc, length_scale, out_scale):
        own_part = kernel_product(x_loc, norm_loc, x_loc, norm_loc, v_loc, length_scale, out_scale)

        def visit_step(step_idx, loop_state):
            x_vis, v_vis, running = loop_state
            x_vis = lax.ppermute(x_vis, "row", shift_pairs)
            v_vis = lax.ppermute(v_vis, "row", shift_pairs)
            norm_vis = jnp.sum(jnp.square(x_vis.astype(jnp.float32)), axis=1)
            running = running + kernel_product(x_loc, norm_loc, x_vis, norm_vis, v_vis, length_scale, out_scale)
            return x_vis, v_vis, running

        final_state = lax.fori_loop(1, n_row, visit_step, (x_loc, v_loc, own_part))
        return final_state[2]

    def local_program(x_loc, v_loc, length_scale, out_scale):
        norm_loc = jnp.sum(jnp.square(x_loc.astype(jnp.float32)), axis=1)
        first_pass = kernel_pass(x_loc, norm_loc, v_loc, length_scale, out_scale).astype(jnp.bfloat16)
        return kernel_pass(x_loc, norm_loc, first_pass, length_scale, out_scale)

    row_spec = P(("task", "row"), None)
    return jax.shard_map(local_program, mesh=mesh, in_specs=(row_spec, row_spec, P("task"), P("task")), out_specs=row_spec, check_vma=False)
```

profile of v0, /device:TPU:112, one launch (start us, length us, event | category | flops | bytes accessed | tf_op | source)
XLA Modules:
  0.0 881.0 jit_solution(6671525437150601952)
XLA Ops:
  27.3 405.7 %while.32 = (s32[]{:T(128)}, bf16[2048,768]{1,0:T(8,128)(2,1)}, bf16[2048,64]{0,1:T(8,128)(2,1)}, f32[2048,64]{0,1:T(8,128)}, f32[1]{0:T(128)}, /*index=5*/f32[2...) while((s32[]{:T(128)}, bf16[2048,768]{1,0:T(8,128)(2,1)}, bf16[2048,64]{0,1:T(8,128)(2,1)}, ...), condition=%wide.region_3.0_spmd, body=%wide.region_1.0_spmd.sunk | while | flops 7017723904 | bytes 31219892 | solution.py:28
  29.8 38.7 %collective-permute-done.1 = bf16[2048,64]{0,1:T(8,128)(2,1)S(1)} collective-permute-done((bf16[2048,64]{0,1:T(8,128)(2,1)}, bf16[2048,64]{0,1:T(8,128)(2,1)S(1)}, u32[]{:S(2)}, u32[]{:S(2)}) %collective-permute-start.1) | collective-permute-done | bytes 262176 | tf_op jit(solution)/shard_map/while/body/eval_jaxpr/ppermute | solution.py:23
  86.5 39.9 %collective-permute-done.1 = bf16[2048,64]{0,1:T(8,128)(2,1)S(1)} collective-permute-done((bf16[2048,64]{0,1:T(8,128)(2,1)}, bf16[2048,64]{0,1:T(8,128)(2,1)S(1)}, u32[]{:S(2)}, u32[]{:S(2)}) %collective-permute-start.1) | collective-permute-done | bytes 262176 | tf_op jit(solution)/shard_map/while/body/eval_jaxpr/ppermute | solution.py:23
  129.5 14.0 %fusion.37 = f32[2048,64]{0,1:T(8,128)} fusion(f32[2048,64]{0,1:T(8,128)} %get-tuple-element.339, bf16[2048,64]{0,1:T(8,128)(2,1)S(1)} %collective-permute-done.1, f32[]{:T(128)} %bitcast.31, f32[2048]{0:T(1024)S(1)} %multiply_reduce_fusion.5, f32[2048]{0:T(1024)S(1)} %get-tuple-element.350, f32[]{:T(128)} %bitcast.32, ...), kind=kOutput, calls=%fused_computation.4.clone.1 | convolution fusion | flops 7013007360 | bytes 7618568 | tf_op jit(solution)/shard_map/while/body/eval_jaxpr/dot_general | solution.py:15
  143.5 40.7 %collective-permute-done.1 = bf16[2048,64]{0,1:T(8,128)(2,1)S(1)} collective-permute-done((bf16[2048,64]{0,1:T(8,128)(2,1)}, bf16[2048,64]{0,1:T(8,128)(2,1)S(1)}, u32[]{:S(2)}, u32[]{:S(2)}) %collective-permute-start.1) | collective-permute-done | bytes 262176 | tf_op jit(solution)/shard_map/while/body/eval_jaxpr/ppermute | solution.py:23
  201.4 40.7 %collective-permute-done.1 = bf16[2048,64]{0,1:T(8,128)(2,1)S(1)} collective-permute-done((bf16[2048,64]{0,1:T(8,128)(2,1)}, bf16[2048,64]{0,1:T(8,128)(2,1)S(1)}, u32[]{:S(2)}, u32[]{:S(2)}) %collective-permute-start.1) | collective-permute-done | bytes 262176 | tf_op jit(solution)/shard_map/while/body/eval_jaxpr/ppermute | solution.py:23
  259.3 40.7 %collective-permute-done.1 = bf16[2048,64]{0,1:T(8,128)(2,1)S(1)} collective-permute-done((bf16[2048,64]{0,1:T(8,128)(2,1)}, bf16[2048,64]{0,1:T(8,128)(2,1)S(1)}, u32[]{:S(2)}, u32[]{:S(2)}) %collective-permute-start.1) | collective-permute-done | bytes 262176 | tf_op jit(solution)/shard_map/while/body/eval_jaxpr/ppermute | solution.py:23
  317.2 40.7 %collective-permute-done.1 = bf16[2048,64]{0,1:T(8,128)(2,1)S(1)} collective-permute-done((bf16[2048,64]{0,1:T(8,128)(2,1)}, bf16[2048,64]{0,1:T(8,128)(2,1)S(1)}, u32[]{:S(2)}, u32[]{:S(2)}) %collective-permute-start.1) | collective-permute-done | bytes 262176 | tf_op jit(solution)/shard_map/while/body/eval_jaxpr/ppermute | solution.py:23
  375.1 40.7 %collective-permute-done.1 = bf16[2048,64]{0,1:T(8,128)(2,1)S(1)} collective-permute-done((bf16[2048,64]{0,1:T(8,128)(2,1)}, bf16[2048,64]{0,1:T(8,128)(2,1)S(1)}, u32[]{:S(2)}, u32[]{:S(2)}) %collective-permute-start.1) | collective-permute-done | bytes 262176 | tf_op jit(solution)/shard_map/while/body/eval_jaxpr/ppermute | solution.py:23
  445.8 435.3 %while.33 = (s32[]{:T(128)}, bf16[2048,768]{1,0:T(8,128)(2,1)}, bf16[2048,64]{1,0:T(8,128)(2,1)}, f32[2048,64]{0,1:T(8,128)}, f32[1]{0:T(128)}, /*index=5*/f32[2...) while((s32[]{:T(128)}, bf16[2048,768]{1,0:T(8,128)(2,1)}, bf16[2048,64]{1,0:T(8,128)(2,1)}, ...), condition=%wide.region_6.0_spmd, body=%wide.region_4.0_spmd.sunk | while | flops 7017723904 | bytes 31219892 | solution.py:28
  445.8 43.5 %collective-permute-done.3 = bf16[2048,64]{1,0:T(8,128)(2,1)} collective-permute-done((bf16[2048,64]{1,0:T(8,128)(2,1)}, bf16[2048,64]{1,0:T(8,128)(2,1)}, u32[]{:S(2)}, u32[]{:S(2)}) %collective-permute-start.3) | collective-permute-done | bytes 262176 | tf_op jit(solution)/shard_map/while/body/eval_jaxpr/ppermute | solution.py:23
  493.6 14.4 %fusion.41 = f32[2048,64]{0,1:T(8,128)} fusion(f32[2048,64]{0,1:T(8,128)} %get-tuple-element.366, bf16[2048,64]{1,0:T(8,128)(2,1)} %collective-permute-done.3, f32[]{:T(128)} %bitcast.36, f32[2048]{0:T(1024)S(1)} %multiply_reduce_fusion.6, f32[2048]{0:T(1024)S(1)} %get-tuple-element.377, f32[]{:T(128)} %bitcast.37, ...), kind=kOutput, calls=%fused_computation.11.clone.1 | convolution fusion | flops 7013007360 | bytes 7618568 | tf_op jit(solution)/shard_map/while/body/eval_jaxpr/dot_general | solution.py:15
  507.9 43.5 %collective-permute-done.3 = bf16[2048,64]{1,0:T(8,128)(2,1)} collective-permute-done((bf16[2048,64]{1,0:T(8,128)(2,1)}, bf16[2048,64]{1,0:T(8,128)(2,1)}, u32[]{:S(2)}, u32[]{:S(2)}) %collective-permute-start.3) | collective-permute-done | bytes 262176 | tf_op jit(solution)/shard_map/while/body/eval_jaxpr/ppermute | solution.py:23
  555.7 14.4 %fusion.41 = f32[2048,64]{0,1:T(8,128)} fusion(f32[2048,64]{0,1:T(8,128)} %get-tuple-element.366, bf16[2048,64]{1,0:T(8,128)(2,1)} %collective-permute-done.3, f32[]{:T(128)} %bitcast.36, f32[2048]{0:T(1024)S(1)} %multiply_reduce_fusion.6, f32[2048]{0:T(1024)S(1)} %get-tuple-element.377, f32[]{:T(128)} %bitcast.37, ...), kind=kOutput, calls=%fused_computation.11.clone.1 | convolution fusion | flops 7013007360 | bytes 7618568 | tf_op jit(solution)/shard_map/while/body/eval_jaxpr/dot_general | solution.py:15
  570.1 43.5 %collective-permute-done.3 = bf16[2048,64]{1,0:T(8,128)(2,1)} collective-permute-done((bf16[2048,64]{1,0:T(8,128)(2,1)}, bf16[2048,64]{1,0:T(8,128)(2,1)}, u32[]{:S(2)}, u32[]{:S(2)}) %collective-permute-start.3) | collective-permute-done | bytes 262176 | tf_op jit(solution)/shard_map/while/body/eval_jaxpr/ppermute | solution.py:23
  617.9 14.4 %fusion.41 = f32[2048,64]{0,1:T(8,128)} fusion(f32[2048,64]{0,1:T(8,128)} %get-tuple-element.366, bf16[2048,64]{1,0:T(8,128)(2,1)} %collective-permute-done.3, f32[]{:T(128)} %bitcast.36, f32[2048]{0:T(1024)S(1)} %multiply_reduce_fusion.6, f32[2048]{0:T(1024)S(1)} %get-tuple-element.377, f32[]{:T(128)} %bitcast.37, ...), kind=kOutput, calls=%fused_computation.11.clone.1 | convolution fusion | flops 7013007360 | bytes 7618568 | tf_op jit(solution)/shard_map/while/body/eval_jaxpr/dot_general | solution.py:15
  632.3 43.5 %collective-permute-done.3 = bf16[2048,64]{1,0:T(8,128)(2,1)} collective-permute-done((bf16[2048,64]{1,0:T(8,128)(2,1)}, bf16[2048,64]{1,0:T(8,128)(2,1)}, u32[]{:S(2)}, u32[]{:S(2)}) %collective-permute-start.3) | collective-permute-done | bytes 262176 | tf_op jit(solution)/shard_map/while/body/eval_jaxpr/ppermute | solution.py:23
  680.1 14.4 %fusion.41 = f32[2048,64]{0,1:T(8,128)} fusion(f32[2048,64]{0,1:T(8,128)} %get-tuple-element.366, bf16[2048,64]{1,0:T(8,128)(2,1)} %collective-permute-done.3, f32[]{:T(128)} %bitcast.36, f32[2048]{0:T(1024)S(1)} %multiply_reduce_fusion.6, f32[2048]{0:T(1024)S(1)} %get-tuple-element.377, f32[]{:T(128)} %bitcast.37, ...), kind=kOutput, calls=%fused_computation.11.clone.1 | convolution fusion | flops 7013007360 | bytes 7618568 | tf_op jit(solution)/shard_map/while/body/eval_jaxpr/dot_general | solution.py:15
  694.5 43.5 %collective-permute-done.3 = bf16[2048,64]{1,0:T(8,128)(2,1)} collective-permute-done((bf16[2048,64]{1,0:T(8,128)(2,1)}, bf16[2048,64]{1,0:T(8,128)(2,1)}, u32[]{:S(2)}, u32[]{:S(2)}) %collective-permute-start.3) | collective-permute-done | bytes 262176 | tf_op jit(solution)/shard_map/while/body/eval_jaxpr/ppermute | solution.py:23
  742.3 14.4 %fusion.41 = f32[2048,64]{0,1:T(8,128)} fusion(f32[2048,64]{0,1:T(8,128)} %get-tuple-element.366, bf16[2048,64]{1,0:T(8,128)(2,1)} %collective-permute-done.3, f32[]{:T(128)} %bitcast.36, f32[2048]{0:T(1024)S(1)} %multiply_reduce_fusion.6, f32[2048]{0:T(1024)S(1)} %get-tuple-element.377, f32[]{:T(128)} %bitcast.37, ...), kind=kOutput, calls=%fused_computation.11.clone.1 | convolution fusion | flops 7013007360 | bytes 7618568 | tf_op jit(solution)/shard_map/while/body/eval_jaxpr/dot_general | solution.py:15
  756.7 43.5 %collective-permute-done.3 = bf16[2048,64]{1,0:T(8,128)(2,1)} collective-permute-done((bf16[2048,64]{1,0:T(8,128)(2,1)}, bf16[2048,64]{1,0:T(8,128)(2,1)}, u32[]{:S(2)}, u32[]{:S(2)}) %collective-permute-start.3) | collective-permute-done | bytes 262176 | tf_op jit(solution)/shard_map/while/body/eval_jaxpr/ppermute | solution.py:23
  804.5 14.4 %fusion.41 = f32[2048,64]{0,1:T(8,128)} fusion(f32[2048,64]{0,1:T(8,128)} %get-tuple-element.366, bf16[2048,64]{1,0:T(8,128)(2,1)} %collective-permute-done.3, f32[]{:T(128)} %bitcast.36, f32[2048]{0:T(1024)S(1)} %multiply_reduce_fusion.6, f32[2048]{0:T(1024)S(1)} %get-tuple-element.377, f32[]{:T(128)} %bitcast.37, ...), kind=kOutput, calls=%fused_computation.11.clone.1 | convolution fusion | flops 7013007360 | bytes 7618568 | tf_op jit(solution)/shard_map/while/body/eval_jaxpr/dot_general | solution.py:15
  818.8 43.5 %collective-permute-done.3 = bf16[2048,64]{1,0:T(8,128)(2,1)} collective-permute-done((bf16[2048,64]{1,0:T(8,128)(2,1)}, bf16[2048,64]{1,0:T(8,128)(2,1)}, u32[]{:S(2)}, u32[]{:S(2)}) %collective-permute-start.3) | collective-permute-done | bytes 262176 | tf_op jit(solution)/shard_map/while/body/eval_jaxpr/ppermute | solution.py:23
  866.6 14.4 %fusion.41 = f32[2048,64]{0,1:T(8,128)} fusion(f32[2048,64]{0,1:T(8,128)} %get-tuple-element.366, bf16[2048,64]{1,0:T(8,128)(2,1)} %collective-permute-done.3, f32[]{:T(128)} %bitcast.36, f32[2048]{0:T(1024)S(1)} %multiply_reduce_fusion.6, f32[2048]{0:T(1024)S(1)} %get-tuple-element.377, f32[]{:T(128)} %bitcast.37, ...), kind=kOutput, calls=%fused_computation.11.clone.1 | convolution fusion | flops 7013007360 | bytes 7618568 | tf_op jit(solution)/shard_map/while/body/eval_jaxpr/dot_general | solution.py:15
  (102 shorter events, 178.1 us)
Async XLA Ops:
  27.3 41.9 %collective-permute-start = (bf16[2048,768]{1,0:T(8,128)(2,1)}, bf16[2048,768]{1,0:T(8,128)(2,1)S(1)}, u32[]{:S(2)}, u32[]{:S(2)}) collective-permute-start(bf16[2048,768]{1,0:T(8,128)(2,1)} %get-tuple-element.337), channel_id=1, source_target_pairs={{0,1},{1,2},{2,3},{3,4},{4,5},{5,6},{6,7},{7,0},{8,9},{9,10},{10,1... | collective-permute-start | bytes 9437192 | tf_op jit(solution)/shard_map/while/body/eval_jaxpr/ppermute | solution.py:22
  27.3 41.2 %collective-permute-start.1 = (bf16[2048,64]{0,1:T(8,128)(2,1)}, bf16[2048,64]{0,1:T(8,128)(2,1)S(1)}, u32[]{:S(2)}, u32[]{:S(2)}) collective-permute-start(bf16[2048,64]{0,1:T(8,128)(2,1)} %get-tuple-element.338), channel_id=1, source_target_pairs={{0,1},{1,2},{2,3},{3,4},{4,5},{5,6},{6,7},{7,0},{8,9},{9,10},{10,1... | collective-permute-start | bytes 786440 | tf_op jit(solution)/shard_map/while/body/eval_jaxpr/ppermute | solution.py:23
  85.6 41.4 %collective-permute-start = (bf16[2048,768]{1,0:T(8,128)(2,1)}, bf16[2048,768]{1,0:T(8,128)(2,1)S(1)}, u32[]{:S(2)}, u32[]{:S(2)}) collective-permute-start(bf16[2048,768]{1,0:T(8,128)(2,1)} %get-tuple-element.337), channel_id=1, source_target_pairs={{0,1},{1,2},{2,3},{3,4},{4,5},{5,6},{6,7},{7,0},{8,9},{9,10},{10,1... | collective-permute-start | bytes 9437192 | tf_op jit(solution)/shard_map/while/body/eval_jaxpr/ppermute | solution.py:22
  85.6 40.7 %collective-permute-start.1 = (bf16[2048,64]{0,1:T(8,128)(2,1)}, bf16[2048,64]{0,1:T(8,128)(2,1)S(1)}, u32[]{:S(2)}, u32[]{:S(2)}) collective-permute-start(bf16[2048,64]{0,1:T(8,128)(2,1)} %get-tuple-element.338), channel_id=1, source_target_pairs={{0,1},{1,2},{2,3},{3,4},{4,5},{5,6},{6,7},{7,0},{8,9},{9,10},{10,1... | collective-permute-start | bytes 786440 | tf_op jit(solution)/shard_map/while/body/eval_jaxpr/ppermute | solution.py:23
  143.5 41.4 %collective-permute-start = (bf16[2048,768]{1,0:T(8,128)(2,1)}, bf16[2048,768]{1,0:T(8,128)(2,1)S(1)}, u32[]{:S(2)}, u32[]{:S(2)}) collective-permute-start(bf16[2048,768]{1,0:T(8,128)(2,1)} %get-tuple-element.337), channel_id=1, source_target_pairs={{0,1},{1,2},{2,3},{3,4},{4,5},{5,6},{6,7},{7,0},{8,9},{9,10},{10,1... | collective-permute-start | bytes 9437192 | tf_op jit(solution)/shard_map/while/body/eval_jaxpr/ppermute | solution.py:22
  201.4 41.4 %collective-permute-start = (bf16[2048,768]{1,0:T(8,128)(2,1)}, bf16[2048,768]{1,0:T(8,128)(2,1)S(1)}, u32[]{:S(2)}, u32[]{:S(2)}) collective-permute-start(bf16[2048,768]{1,0:T(8,128)(2,1)} %get-tuple-element.337), channel_id=1, source_target_pairs={{0,1},{1,2},{2,3},{3,4},{4,5},{5,6},{6,7},{7,0},{8,9},{9,10},{10,1... | collective-permute-start | bytes 9437192 | tf_op jit(solution)/shard_map/while/body/eval_jaxpr/ppermute | solution.py:22
  259.3 41.4 %collective-permute-start = (bf16[2048,768]{1,0:T(8,128)(2,1)}, bf16[2048,768]{1,0:T(8,128)(2,1)S(1)}, u32[]{:S(2)}, u32[]{:S(2)}) collective-permute-start(bf16[2048,768]{1,0:T(8,128)(2,1)} %get-tuple-element.337), channel_id=1, source_target_pairs={{0,1},{1,2},{2,3},{3,4},{4,5},{5,6},{6,7},{7,0},{8,9},{9,10},{10,1... | collective-permute-start | bytes 9437192 | tf_op jit(solution)/shard_map/while/body/eval_jaxpr/ppermute | solution.py:22
  259.3 40.7 %collective-permute-start.1 = (bf16[2048,64]{0,1:T(8,128)(2,1)}, bf16[2048,64]{0,1:T(8,128)(2,1)S(1)}, u32[]{:S(2)}, u32[]{:S(2)}) collective-permute-start(bf16[2048,64]{0,1:T(8,128)(2,1)} %get-tuple-element.338), channel_id=1, source_target_pairs={{0,1},{1,2},{2,3},{3,4},{4,5},{5,6},{6,7},{7,0},{8,9},{9,10},{10,1... | collective-permute-start | bytes 786440 | tf_op jit(solution)/shard_map/while/body/eval_jaxpr/ppermute | solution.py:23
  317.2 41.4 %collective-permute-start = (bf16[2048,768]{1,0:T(8,128)(2,1)}, bf16[2048,768]{1,0:T(8,128)(2,1)S(1)}, u32[]{:S(2)}, u32[]{:S(2)}) collective-permute-start(bf16[2048,768]{1,0:T(8,128)(2,1)} %get-tuple-element.337), channel_id=1, source_target_pairs={{0,1},{1,2},{2,3},{3,4},{4,5},{5,6},{6,7},{7,0},{8,9},{9,10},{10,1... | collective-permute-start | bytes 9437192 | tf_op jit(solution)/shard_map/while/body/eval_jaxpr/ppermute | solution.py:22
  375.1 41.4 %collective-permute-start = (bf16[2048,768]{1,0:T(8,128)(2,1)}, bf16[2048,768]{1,0:T(8,128)(2,1)S(1)}, u32[]{:S(2)}, u32[]{:S(2)}) collective-permute-start(bf16[2048,768]{1,0:T(8,128)(2,1)} %get-tuple-element.337), channel_id=1, source_target_pairs={{0,1},{1,2},{2,3},{3,4},{4,5},{5,6},{6,7},{7,0},{8,9},{9,10},{10,1... | collective-permute-start | bytes 9437192 | tf_op jit(solution)/shard_map/while/body/eval_jaxpr/ppermute | solution.py:22
  445.8 45.4 %collective-permute-start.2 = (bf16[2048,768]{1,0:T(8,128)(2,1)}, bf16[2048,768]{1,0:T(8,128)(2,1)S(1)}, u32[]{:S(2)}, u32[]{:S(2)}) collective-permute-start(bf16[2048,768]{1,0:T(8,128)(2,1)} %get-tuple-element.364), channel_id=1, source_target_pairs={{0,1},{1,2},{2,3},{3,4},{4,5},{5,6},{6,7},{7,0},{8,9},{9,10},{10,1... | collective-permute-start | bytes 9437192 | tf_op jit(solution)/shard_map/while/body/eval_jaxpr/ppermute | solution.py:22
  445.8 43.5 %collective-permute-start.3 = (bf16[2048,64]{1,0:T(8,128)(2,1)}, bf16[2048,64]{1,0:T(8,128)(2,1)}, u32[]{:S(2)}, u32[]{:S(2)}) collective-permute-start(bf16[2048,64]{1,0:T(8,128)(2,1)} %get-tuple-element.365), channel_id=1, source_target_pairs={{0,1},{1,2},{2,3},{3,4},{4,5},{5,6},{6,7},{7,0},{8,9},{9,10},{10,1... | collective-permute-start | bytes 786440 | tf_op jit(solution)/shard_map/while/body/eval_jaxpr/ppermute | solution.py:23
  507.9 45.4 %collective-permute-start.2 = (bf16[2048,768]{1,0:T(8,128)(2,1)}, bf16[2048,768]{1,0:T(8,128)(2,1)S(1)}, u32[]{:S(2)}, u32[]{:S(2)}) collective-permute-start(bf16[2048,768]{1,0:T(8,128)(2,1)} %get-tuple-element.364), channel_id=1, source_target_pairs={{0,1},{1,2},{2,3},{3,4},{4,5},{5,6},{6,7},{7,0},{8,9},{9,10},{10,1... | collective-permute-start | bytes 9437192 | tf_op jit(solution)/shard_map/while/body/eval_jaxpr/ppermute | solution.py:22
  507.9 43.5 %collective-permute-start.3 = (bf16[2048,64]{1,0:T(8,128)(2,1)}, bf16[2048,64]{1,0:T(8,128)(2,1)}, u32[]{:S(2)}, u32[]{:S(2)}) collective-permute-start(bf16[2048,64]{1,0:T(8,128)(2,1)} %get-tuple-element.365), channel_id=1, source_target_pairs={{0,1},{1,2},{2,3},{3,4},{4,5},{5,6},{6,7},{7,0},{8,9},{9,10},{10,1... | collective-permute-start | bytes 786440 | tf_op jit(solution)/shard_map/while/body/eval_jaxpr/ppermute | solution.py:23
  570.1 45.4 %collective-permute-start.2 = (bf16[2048,768]{1,0:T(8,128)(2,1)}, bf16[2048,768]{1,0:T(8,128)(2,1)S(1)}, u32[]{:S(2)}, u32[]{:S(2)}) collective-permute-start(bf16[2048,768]{1,0:T(8,128)(2,1)} %get-tuple-element.364), channel_id=1, source_target_pairs={{0,1},{1,2},{2,3},{3,4},{4,5},{5,6},{6,7},{7,0},{8,9},{9,10},{10,1... | collective-permute-start | bytes 9437192 | tf_op jit(solution)/shard_map/while/body/eval_jaxpr/ppermute | solution.py:22
  570.1 43.5 %collective-permute-start.3 = (bf16[2048,64]{1,0:T(8,128)(2,1)}, bf16[2048,64]{1,0:T(8,128)(2,1)}, u32[]{:S(2)}, u32[]{:S(2)}) collective-permute-start(bf16[2048,64]{1,0:T(8,128)(2,1)} %get-tuple-element.365), channel_id=1, source_target_pairs={{0,1},{1,2},{2,3},{3,4},{4,5},{5,6},{6,7},{7,0},{8,9},{9,10},{10,1... | collective-permute-start | bytes 786440 | tf_op jit(solution)/shard_map/while/body/eval_jaxpr/ppermute | solution.py:23
  632.3 45.4 %collective-permute-start.2 = (bf16[2048,768]{1,0:T(8,128)(2,1)}, bf16[2048,768]{1,0:T(8,128)(2,1)S(1)}, u32[]{:S(2)}, u32[]{:S(2)}) collective-permute-start(bf16[2048,768]{1,0:T(8,128)(2,1)} %get-tuple-element.364), channel_id=1, source_target_pairs={{0,1},{1,2},{2,3},{3,4},{4,5},{5,6},{6,7},{7,0},{8,9},{9,10},{10,1... | collective-permute-start | bytes 9437192 | tf_op jit(solution)/shard_map/while/body/eval_jaxpr/ppermute | solution.py:22
  632.3 43.5 %collective-permute-start.3 = (bf16[2048,64]{1,0:T(8,128)(2,1)}, bf16[2048,64]{1,0:T(8,128)(2,1)}, u32[]{:S(2)}, u32[]{:S(2)}) collective-permute-start(bf16[2048,64]{1,0:T(8,128)(2,1)} %get-tuple-element.365), channel_id=1, source_target_pairs={{0,1},{1,2},{2,3},{3,4},{4,5},{5,6},{6,7},{7,0},{8,9},{9,10},{10,1... | collective-permute-start | bytes 786440 | tf_op jit(solution)/shard_map/while/body/eval_jaxpr/ppermute | solution.py:23
  694.5 45.4 %collective-permute-start.2 = (bf16[2048,768]{1,0:T(8,128)(2,1)}, bf16[2048,768]{1,0:T(8,128)(2,1)S(1)}, u32[]{:S(2)}, u32[]{:S(2)}) collective-permute-start(bf16[2048,768]{1,0:T(8,128)(2,1)} %get-tuple-element.364), channel_id=1, source_target_pairs={{0,1},{1,2},{2,3},{3,4},{4,5},{5,6},{6,7},{7,0},{8,9},{9,10},{10,1... | collective-permute-start | bytes 9437192 | tf_op jit(solution)/shard_map/while/body/eval_jaxpr/ppermute | solution.py:22
  694.5 43.5 %collective-permute-start.3 = (bf16[2048,64]{1,0:T(8,128)(2,1)}, bf16[2048,64]{1,0:T(8,128)(2,1)}, u32[]{:S(2)}, u32[]{:S(2)}) collective-permute-start(bf16[2048,64]{1,0:T(8,128)(2,1)} %get-tuple-element.365), channel_id=1, source_target_pairs={{0,1},{1,2},{2,3},{3,4},{4,5},{5,6},{6,7},{7,0},{8,9},{9,10},{10,1... | collective-permute-start | bytes 786440 | tf_op jit(solution)/shard_map/while/body/eval_jaxpr/ppermute | solution.py:23
  756.7 45.4 %collective-permute-start.2 = (bf16[2048,768]{1,0:T(8,128)(2,1)}, bf16[2048,768]{1,0:T(8,128)(2,1)S(1)}, u32[]{:S(2)}, u32[]{:S(2)}) collective-permute-start(bf16[2048,768]{1,0:T(8,128)(2,1)} %get-tuple-element.364), channel_id=1, source_target_pairs={{0,1},{1,2},{2,3},{3,4},{4,5},{5,6},{6,7},{7,0},{8,9},{9,10},{10,1... | collective-permute-start | bytes 9437192 | tf_op jit(solution)/shard_map/while/body/eval_jaxpr/ppermute | solution.py:22
  756.7 43.5 %collective-permute-start.3 = (bf16[2048,64]{1,0:T(8,128)(2,1)}, bf16[2048,64]{1,0:T(8,128)(2,1)}, u32[]{:S(2)}, u32[]{:S(2)}) collective-permute-start(bf16[2048,64]{1,0:T(8,128)(2,1)} %get-tuple-element.365), channel_id=1, source_target_pairs={{0,1},{1,2},{2,3},{3,4},{4,5},{5,6},{6,7},{7,0},{8,9},{9,10},{10,1... | collective-permute-start | bytes 786440 | tf_op jit(solution)/shard_map/while/body/eval_jaxpr/ppermute | solution.py:23
  818.8 45.4 %collective-permute-start.2 = (bf16[2048,768]{1,0:T(8,128)(2,1)}, bf16[2048,768]{1,0:T(8,128)(2,1)S(1)}, u32[]{:S(2)}, u32[]{:S(2)}) collective-permute-start(bf16[2048,768]{1,0:T(8,128)(2,1)} %get-tuple-element.364), channel_id=1, source_target_pairs={{0,1},{1,2},{2,3},{3,4},{4,5},{5,6},{6,7},{7,0},{8,9},{9,10},{10,1... | collective-permute-start | bytes 9437192 | tf_op jit(solution)/shard_map/while/body/eval_jaxpr/ppermute | solution.py:22
  818.8 43.5 %collective-permute-start.3 = (bf16[2048,64]{1,0:T(8,128)(2,1)}, bf16[2048,64]{1,0:T(8,128)(2,1)}, u32[]{:S(2)}, u32[]{:S(2)}) collective-permute-start(bf16[2048,64]{1,0:T(8,128)(2,1)} %get-tuple-element.365), channel_id=1, source_target_pairs={{0,1},{1,2},{2,3},{3,4},{4,5},{5,6},{6,7},{7,0},{8,9},{9,10},{10,1... | collective-permute-start | bytes 786440 | tf_op jit(solution)/shard_map/while/body/eval_jaxpr/ppermute | solution.py:23
  (6 other events, 181.9 us)
where the time goes:
time: 882 us; the launch traced here: 881 us
  waiting for transfers between devices  587 us (67%)
  matrix products  221 us (25%)
  local copies, waits for them, and re-layouts  56.2 us (6%)
  other arithmetic  12.1 us (1%)
    ppermute x14, waiting for transfers between devices, visit_step(): v_vis = lax.ppermute(v_vis, 'row', shift_pairs)  587 us
    dot_general x16, matrix products, kernel_product(): return jnp.dot(kern_tile, v_cols, preferred_element_type=jnp.float32)  209 us
    while x28, local copies, waits for them, and re-layouts  42.3 us
  transfers between devices with their start and end apart: 28, of which 14 were waited for; matrix products, arithmetic and copies ran while one was open for 2% of the time, Pallas kernels for 0%

commit v1 on v0

v1 whole, which is shorter than its diff:
```python
import functools

import jax
import jax.numpy as jnp
from jax import lax
from jax.experimental import pallas as pl
from jax.experimental.pallas import tpu as pltpu
from jax.sharding import PartitionSpec as P

F32 = jnp.float32
BF16 = jnp.bfloat16
LOG2E = 1.4426950408889634
OWN, PLUS, MINUS, CROSS, SIB = 0, 1, 2, 3, 4
N_BIG, BIG, N_SMALL, SMALL = 3, 512, 2, 256
N_PIECE = N_BIG + N_SMALL


def dot_nn(a, b):
    return lax.dot_general(a, b, (((1,), (0,)), ((), ())), preferred_element_type=F32)


def dot_nt(a, b):
    return lax.dot_general(a, b, (((1,), (1,)), ((), ())), preferred_element_type=F32)


def kernel(n_row, x_hbm, vt_hbm, coef, out_hbm, xb, kb, vb, yb, hr, acc, rb,
           x_s, x_r, f_s, f_r, sib_s, sib_r, loc, v_s, v_r, y_s, y_r, p_s, p_r, free):
    rows = xb.shape[1]
    me = lax.axis_index("row")
    core = me % 2
    sib = me + 1 - 2 * core
    plus = (me + 2) % n_row
    minus = (me + n_row - 2) % n_row
    far = 2 + (me // 2) // 2

    def remote(src, dst, s_sem, r_sem, dev):
        return pltpu.make_async_remote_copy(
            src_ref=src, dst_ref=dst, send_sem=s_sem, recv_sem=r_sem,
            device_id={"row": dev}, device_id_type=pl.DeviceIdType.MESH)

    def x_copy(direction, piece, start, width):
        slot, dev = ((MINUS, plus), (PLUS, minus))[direction]
        return remote(x_hbm.at[pl.ds(start, width)], xb.at[slot, pl.ds(start, width)],
                      x_s.at[direction, piece], x_r.at[direction, piece], dev)

    def forward(piece, start, width):
        return remote(xb.at[MINUS, pl.ds(start, width)], xb.at[CROSS, pl.ds(start, width)],
                      f_s.at[piece], f_r.at[piece], sib)

    def vec_copies(src, buf, s_sem, r_sem):
        return (remote(src, buf.at[MINUS], s_sem.at[0], r_sem.at[0], plus),
                remote(src, buf.at[PLUS], s_sem.at[1], r_sem.at[1], minus),
                remote(src, buf.at[SIB], s_sem.at[2], r_sem.at[2], sib),
                remote(buf.at[MINUS], buf.at[CROSS], s_sem.at[3], r_sem.at[3], sib))

    def part_copies(step):
        return (remote(acc.at[PLUS], rb.at[0], p_s.at[step, 0], p_r.at[step, 0], plus),
                remote(acc.at[MINUS], rb.at[1], p_s.at[step, 1], p_r.at[step, 1], minus),
                remote(acc.at[CROSS], rb.at[2], p_s.at[step, 2], p_r.at[step, 2], sib))

    pieces = [(i, i * BIG, BIG) for i in range(N_BIG)]
    pieces += [(N_BIG + i, N_BIG * BIG + i * SMALL, SMALL) for i in range(N_SMALL)]

    barrier = pltpu.get_barrier_semaphore()
    for dev in (sib, plus, minus):
        pl.semaphore_signal(barrier, inc=1, device_id={"row": dev}, device_id_type=pl.DeviceIdType.MESH)
    pl.semaphore_wait(barrier, 3)

    own_x = pltpu.make_async_copy(x_hbm, xb.at[OWN], loc.at[0])
    own_v = pltpu.make_async_copy(vt_hbm, vb.at[OWN], loc.at[1])
    own_x.start()
    own_v.start()
    v_plus, v_minus, v_sib, v_cross = vec_copies(vt_hbm, vb, v_s, v_r)
    sib_x = remote(x_hbm, xb.at[CROSS], sib_s, sib_r, sib)
    v_plus.start()
    v_minus.start()
    for piece in pieces:
        x_copy(0, *piece).start()
        x_copy(1, *piece).start()
    v_sib.start()
    sib_x.start()

    coef_d = coef[0, 0]
    coef_s = coef[0, 1]
    eye = (lax.broadcasted_iota(jnp.int32, (128, 128), 0) == lax.broadcasted_iota(jnp.int32, (128, 128), 1))

    def half_norms(slot, start, width):
        for sub in range(0, width, 128):
            x_sub = xb[slot, pl.ds(start + sub, 128), :].astype(F32)
            col = jnp.sum(x_sub * x_sub, axis=1, keepdims=True) * 0.5
            hr[slot, :, pl.ds(start + sub, 128)] = jnp.sum(jnp.where(eye, col, 0.0), axis=0, keepdims=True)

    def tile(p_slot, p0, m, q_slot, q0, n, k_slot, v_p, acc_q, v_q=None, acc_p=None):
        gram = dot_nt(xb[p_slot, pl.ds(p0, m), :], xb[q_slot, pl.ds(q0, n), :])
        h_q = hr[q_slot, :, pl.ds(q0, n)]
        for sub in range(0, m, 128):
            h_row = hr[p_slot, :, pl.ds(p0 + sub, 128)]
            h_p = jnp.sum(jnp.where(eye, h_row, 0.0), axis=1, keepdims=True)
            half_d = jnp.maximum(h_p + h_q - gram[sub:sub + 128], 0.0)
            kb[k_slot, pl.ds(p0 + sub, 128), pl.ds(q0, n)] = (coef_s * jnp.exp2(half_d * coef_d)).astype(BF16)
        k_tile = kb[k_slot, pl.ds(p0, m), pl.ds(q0, n)]
        acc[acc_q, :, pl.ds(q0, n)] += dot_nn(vb[v_p, :, pl.ds(p0, m)], k_tile)
        if v_q is not None:
            acc[acc_p, :, pl.ds(p0, m)] += dot_nt(vb[v_q, :, pl.ds(q0, n)], k_tile)

    def mul(i, size):
        return pl.multiple_of(i * size, size)

    acc[...] = jnp.zeros_like(acc)
    own_x.wait()
    own_v.wait()

    def norm_loop(slot):
        @pl.loop(0, rows // 256)
        def _(i):
            half_norms(slot, mul(i, 256), 256)

    norm_loop(OWN)
    side = rows // 512

    @pl.loop(0, side * side)
    def _(i):
        tile(OWN, mul(i // side, 512), 512, OWN, mul(i % side, 512), 512, 0, OWN, OWN)

    sib_x.wait_recv()
    v_sib.wait_recv()
    norm_loop(CROSS)

    @pl.loop(0, side * side)
    def _(i):
        tile(CROSS, mul(i // side, 512), 512, OWN, mul(i % side, 512), 512, 1, SIB, OWN)

    pl.semaphore_signal(free, inc=1, device_id={"row": sib}, device_id_type=pl.DeviceIdType.MESH)
    v_minus.wait_recv()
    v_plus.wait_recv()
    v_cross.start()
    pl.semaphore_wait(free, 1)
    v_cross.wait_recv()

    def own_pairs(q0, n, m):
        @pl.loop(0, rows // m)
        def _(i):
            tile(OWN, mul(i, m), m, PLUS, q0, n, 2, OWN, PLUS, PLUS, OWN)

    def own_cross(q0, n, m):
        @pl.loop(0, rows // m)
        def _(i):
            tile(OWN, mul(i, m), m, CROSS, q0, n, 3, OWN, CROSS, CROSS, OWN)

    def far_tile(p0, m, q0, n):
        tile(PLUS, p0, m, far, q0, n, 4, PLUS, far, far, PLUS)

    def arrive(piece, start, width, m):
        x_copy(0, piece, start, width).wait_recv()
        forward(piece, start, width).start()
        x_copy(1, piece, start, width).wait_recv()
        for sub in range(0, width, 256):
            half_norms(PLUS, start + sub, 256)
            half_norms(MINUS, start + sub, 256)
        own_pairs(start, width, m)
        forward(piece, start, width).wait_recv()
        for sub in range(0, width, 256):
            half_norms(CROSS, start + sub, 256)
        own_cross(start, width, m)

    @pl.loop(0, N_BIG)
    def _(j):
        start = mul(j, BIG)
        arrive(j, start, BIG, 512)

        @pl.loop(0, j)
        def _(i):
            far_tile(mul(i, BIG), BIG, start, BIG)

        @pl.loop(0, j + 1)
        def _(i):
            far_tile(start, BIG, mul(i, BIG), BIG)

    @pl.loop(0, N_SMALL)
    def _(j):
        start = pl.multiple_of(N_BIG * BIG + j * SMALL, SMALL)
        arrive(N_BIG + j, start, SMALL, 1024)

        @pl.loop(0, N_BIG)
        def _(i):
            far_tile(mul(i, BIG), BIG, start, SMALL)

        @pl.loop(0, N_BIG)
        def _(i):
            far_tile(start, SMALL, mul(i, BIG), BIG)

    far_tile(N_BIG * BIG, N_SMALL * SMALL, N_BIG * BIG, N_SMALL * SMALL)

    def exchange(step):
        to_plus, to_minus, to_sib = part_copies(step)
        to_sib.start()
        to_plus.start()
        to_sib.wait_recv()
        acc[MINUS] += rb[2]
        to_minus.start()
        return to_plus, to_minus, to_sib

    copies = exchange(0)
    copies[0].wait_recv()
    copies[1].wait_recv()
    yb[OWN] = (acc[OWN] + rb[0] + rb[1]).astype(BF16)
    y_plus, y_minus, y_sib, y_cross = vec_copies(yb.at[OWN], yb, y_s, y_r)
    y_plus.start()
    y_minus.start()
    y_sib.start()
    for copy in copies:
        copy.wait_send()
    acc[...] = jnp.zeros_like(acc)

    half = rows // 2

    def apply_nn(k_slot, y_slot, out):
        for q0 in (0, half):
            acc[out, :, pl.ds(q0, half)] += dot_nn(yb[y_slot], kb[k_slot, :, pl.ds(q0, half)])

    def apply_nt(k_slot, y_slot, out):
        for p0 in (0, half):
            acc[out, :, pl.ds(p0, half)] += dot_nt(yb[y_slot], kb[k_slot, pl.ds(p0, half), :])

    @pl.loop(0, 3)
    def _(i):
        apply_nn((2 + i) % 4, OWN, (1 + 2 * i) % 5)

    y_sib.wait_recv()
    apply_nn(1, SIB, OWN)
    y_plus.wait_recv()
    y_cross.start()
    y_minus.wait_recv()
    apply_nn(4, PLUS, far)
    y_cross.wait_recv()
    apply_nt(4, far, PLUS)
    to_plus, to_minus, to_sib = exchange(1)

    @pl.loop(0, 2)
    def _(i):
        apply_nt(2 + i, 1 + 2 * i, OWN)

    to_plus.wait_recv()
    to_minus.wait_recv()
    acc[OWN] += rb[0] + rb[1]
    out_copy = pltpu.make_async_copy(acc.at[OWN], out_hbm, loc.at[0])
    out_copy.start()
    for copy in (to_plus, to_minus, to_sib, y_plus, y_minus, y_sib, y_cross, v_plus, v_minus, v_sib, v_cross, sib_x):
        copy.wait_send()
    for piece in pieces:
        x_copy(0, *piece).wait_send()
        x_copy(1, *piece).wait_send()
        forward(*piece).wait_send()
    out_copy.wait()


def solution(mesh):
    n_row = mesh.shape["row"]
    assert n_row == 8

    def local_program(x_loc, v_loc, length_scale, out_scale):
        rows, feat = x_loc.shape
        cols = v_loc.shape[1]
        coef = jnp.stack([-LOG2E / (length_scale[0] * length_scale[0]), out_scale[0]]).reshape(1, 2)
        dma = pltpu.SemaphoreType.DMA
        out = pl.pallas_call(
            functools.partial(kernel, n_row),
            out_shape=jax.ShapeDtypeStruct((cols, rows), F32),
            in_specs=[pl.BlockSpec(memory_space=pl.ANY), pl.BlockSpec(memory_space=pl.ANY),
                      pl.BlockSpec(memory_space=pltpu.SMEM)],
            out_specs=pl.BlockSpec(memory_space=pl.ANY),
            scratch_shapes=[
                pltpu.VMEM((4, rows, feat), BF16),
                pltpu.VMEM((5, rows, rows), BF16),
                pltpu.VMEM((5, cols, rows), BF16),
                pltpu.VMEM((5, cols, rows), BF16),
                pltpu.VMEM((4, 1, rows), F32),
                pltpu.VMEM((4, cols, rows), F32),
                pltpu.VMEM((3, cols, rows), F32),
                dma((2, N_PIECE)), dma((2, N_PIECE)), dma((N_PIECE,)), dma((N_PIECE,)),
                dma, dma, dma((2,)), dma((4,)), dma((4,)), dma((4,)), dma((4,)),
                dma((2, 3)), dma((2, 3)), pltpu.SemaphoreType.REGULAR,
            ],
            compiler_params=pltpu.CompilerParams(
                collective_id=0, has_side_effects=True, vmem_limit_bytes=67043328),
        )(x_loc, v_loc.T, coef)
        return out.T

    row_spec = P(("task", "row"), None)
    return jax.shard_map(local_program, mesh=mesh, in_specs=(row_spec, row_spec, P("task"), P("task")),
                         out_specs=row_spec, check_vma=False)
```

time: 882 us -> 147 us (0.17)
  waiting for transfers between devices: 587 us -> 0 us
  matrix products: 221 us -> 0 us
  Pallas kernels: 0 us -> 143 us
  local copies, waits for them, and re-layouts: 56.2 us -> 1.87 us
  other arithmetic: 12.1 us -> 0.59 us
    ppermute x28 -> x0, waiting for transfers between devices: 587 us -> none  [the longest x14 587 us: visit_step(): v_vis = lax.ppermute(v_vis, 'row', shift_pairs)]
    dot_general x17 -> x0, matrix products: 221 us -> none  [the longest x16 209 us: kernel_product(): return jnp.dot(kern_tile, v_cols, preferred_element_type=jnp.float32)]
    pallas_call x0 -> x1, Pallas kernels: none -> 143 us  [local_program(): pl.pallas_call(functools.partial(kernel, n_row), out_shape=jax.ShapeDtype...]
    while x29 -> x0, local copies, waits for them, and re-layouts: 44.4 us -> none
    reduce_sum x15 -> x0, other arithmetic: 12.1 us -> none  [the longest x14 9.56 us: visit_step(): norm_vis = jnp.sum(jnp.square(x_vis.astype(jnp.float32)), axis=1)]
    unnamed x7 -> x1, local copies, waits for them, and re-layouts: 11.8 us -> 1.87 us
  transfers between devices with their start and end apart: 28 -> 0, of which waited for: 14 -> 0; matrix products, arithmetic and copies ran while one was open for 2% -> 0% of each run, Pallas kernels for 0% -> 0%
where the time goes in v1:
time: 147 us
  Pallas kernels  143 us (97%)
  local copies, waits for them, and re-layouts  1.87 us (1%)
    pallas_call x1, Pallas kernels, local_program(): pl.pallas_call(functools.partial(kernel, n_row), out_shape=jax.ShapeDtype...  143 us

profile of v1, /device:TPU:112, one launch (start us, length us, event | category | flops | bytes accessed | tf_op | source)
XLA Modules:
  0.0 146.8 jit_solution(4788862508056893158)
XLA Ops:
  1.3 0.6 maximum_bitcast_fusion.coef
  1.9 143.0 %shard_map.46 = f32[64,2048]{1,0:T(8,128)} custom-call(bf16[2048,768]{1,0:T(8,128)(2,1)} %x_hbm.1, bf16[64,2048]{1,0:T(8,128)(2,1)} %bitcast.5, f32[1,2]{1,0:T(1,128)} %maximum_bitcast_fusion.coef), custom_call_target="tpu_custom_call" | custom-call | tf_op jit(solution)/shard_map/pallas_call | solution.py:266
  144.9 1.9 %copy.8 = f32[2048,64]{0,1:T(8,128)} copy(f32[2048,64]{0,1:T(8,128)} %bitcast.4) | data formatting | bytes 1048576

commit v2 on v1

--- a/solution.py
+++ b/solution.py
@@ -11,8 +11,9 @@
 BF16 = jnp.bfloat16
 LOG2E = 1.4426950408889634
 OWN, PLUS, MINUS, CROSS, SIB = 0, 1, 2, 3, 4
-N_BIG, BIG, N_SMALL, SMALL = 3, 512, 2, 256
-N_PIECE = N_BIG + N_SMALL
+TRASH = 4
+T = 512
+N_PIECE = 4
 
 
 def dot_nn(a, b):
@@ -58,8 +59,7 @@
                 remote(acc.at[MINUS], rb.at[1], p_s.at[step, 1], p_r.at[step, 1], minus),
                 remote(acc.at[CROSS], rb.at[2], p_s.at[step, 2], p_r.at[step, 2], sib))
 
-    pieces = [(i, i * BIG, BIG) for i in range(N_BIG)]
-    pieces += [(N_BIG + i, N_BIG * BIG + i * SMALL, SMALL) for i in range(N_SMALL)]
+    pieces = [(i, i * T, T) for i in range(N_PIECE)]
 
     barrier = pltpu.get_barrier_semaphore()
     for dev in (sib, plus, minus):
@@ -90,18 +90,42 @@
             col = jnp.sum(x_sub * x_sub, axis=1, keepdims=True) * 0.5
             hr[slot, :, pl.ds(start + sub, 128)] = jnp.sum(jnp.where(eye, col, 0.0), axis=0, keepdims=True)
 
-    def tile(p_slot, p0, m, q_slot, q0, n, k_slot, v_p, acc_q, v_q=None, acc_p=None):
-        gram = dot_nt(xb[p_slot, pl.ds(p0, m), :], xb[q_slot, pl.ds(q0, n), :])
-        h_q = hr[q_slot, :, pl.ds(q0, n)]
-        for sub in range(0, m, 128):
+    def products(pend, both):
+        k_slot, p0, q0, v_p, acc_q, v_q, acc_p = pend
+        k_tile = kb[k_slot, pl.ds(p0, T), pl.ds(q0, T)]
+        acc[acc_q, :, pl.ds(q0, T)] += dot_nn(vb[v_p, :, pl.ds(p0, T)], k_tile)
+        if both:
+            acc[acc_p, :, pl.ds(p0, T)] += dot_nt(vb[v_q, :, pl.ds(q0, T)], k_tile)
+
+    def tile(p_slot, p0, q_slot, q0, k_slot, pend, both):
+        gram = dot_nt(xb[p_slot, pl.ds(p0, T), :], xb[q_slot, pl.ds(q0, T), :])
+        products(pend, both)
+        h_q = hr[q_slot, :, pl.ds(q0, T)]
+        for sub in range(0, T, 128):
             h_row = hr[p_slot, :, pl.ds(p0 + sub, 128)]
             h_p = jnp.sum(jnp.where(eye, h_row, 0.0), axis=1, keepdims=True)
             half_d = jnp.maximum(h_p + h_q - gram[sub:sub + 128], 0.0)
-            kb[k_slot, pl.ds(p0 + sub, 128), pl.ds(q0, n)] = (coef_s * jnp.exp2(half_d * coef_d)).astype(BF16)
-        k_tile = kb[k_slot, pl.ds(p0, m), pl.ds(q0, n)]
-        acc[acc_q, :, pl.ds(q0, n)] += dot_nn(vb[v_p, :, pl.ds(p0, m)], k_tile)
-        if v_q is not None:
-            acc[acc_p, :, pl.ds(p0, m)] += dot_nt(vb[v_q, :, pl.ds(q0, n)], k_tile)
+            kb[k_slot, pl.ds(p0 + sub, 128), pl.ds(q0, T)] = (coef_s * jnp.exp2(half_d * coef_d)).astype(BF16)
+
+    def tiles(count, place, pend, p_slot, q_slot, k_slot, v_p, acc_q, v_q, acc_p, both=True, unroll=1):
+        def one(i, pend):
+            p_i, q_i = place(i)
+            p0, q0 = mul(p_i, T), mul(q_i, T)
+            pend = (pend[0], pl.multiple_of(pend[1], T), pl.multiple_of(pend[2], T)) + tuple(pend[3:])
+            tile(p_slot, p0, q_slot, q0, k_slot, pend, both)
+            return tuple(jnp.int32(v) for v in (k_slot, p0, q0, v_p, acc_q, v_q, acc_p))
+
+        def step(i, pend):
+            for sub in range(unroll):
+                pend = one(i * unroll + sub, pend)
+            return pend
+
+        return lax.fori_loop(0, count // unroll, step, pend)
+
+    def flush(pend, both):
+        products((pend[0], pl.multiple_of(pend[1], T), pl.multiple_of(pend[2], T)) + tuple(pend[3:]), both)
+
+    nothing = tuple(jnp.int32(v) for v in (0, 0, 0, OWN, TRASH, OWN, TRASH))
 
     def mul(i, size):
         return pl.multiple_of(i * size, size)
@@ -116,20 +140,15 @@
             half_norms(slot, mul(i, 256), 256)
 
     norm_loop(OWN)
-    side = rows // 512
-
-    @pl.loop(0, side * side)
-    def _(i):
-        tile(OWN, mul(i // side, 512), 512, OWN, mul(i % side, 512), 512, 0, OWN, OWN)
+    side = rows // T
+    pend = tiles(side * side, lambda i: (i // side, i % side), nothing, OWN, OWN, 0, OWN, OWN, OWN, TRASH, False, 4)
 
     sib_x.wait_recv()
     v_sib.wait_recv()
     norm_loop(CROSS)
 
-    @pl.loop(0, side * side)
-    def _(i):
-        tile(CROSS, mul(i // side, 512), 512, OWN, mul(i % side, 512), 512, 1, SIB, OWN)
-
+    pend = tiles(side * side, lambda i: (i // side, i % side), pend, CROSS, OWN, 1, SIB, OWN, OWN, TRASH, False, 4)
+    flush(pend, False)
     pl.semaphore_signal(free, inc=1, device_id={"row": sib}, device_id_type=pl.DeviceIdType.MESH)
     v_minus.wait_recv()
     v_plus.wait_recv()
@@ -137,59 +156,23 @@
     pl.semaphore_wait(free, 1)
     v_cross.wait_recv()
 
-    def own_pairs(q0, n, m):
-        @pl.loop(0, rows // m)
-        def _(i):
-            tile(OWN, mul(i, m), m, PLUS, q0, n, 2, OWN, PLUS, PLUS, OWN)
-
-    def own_cross(q0, n, m):
-        @pl.loop(0, rows // m)
-        def _(i):
-            tile(OWN, mul(i, m), m, CROSS, q0, n, 3, OWN, CROSS, CROSS, OWN)
-
-    def far_tile(p0, m, q0, n):
-        tile(PLUS, p0, m, far, q0, n, 4, PLUS, far, far, PLUS)
-
-    def arrive(piece, start, width, m):
-        x_copy(0, piece, start, width).wait_recv()
-        forward(piece, start, width).start()
-        x_copy(1, piece, start, width).wait_recv()
-        for sub in range(0, width, 256):
-            half_norms(PLUS, start + sub, 256)
-            half_norms(MINUS, start + sub, 256)
-        own_pairs(start, width, m)
-        forward(piece, start, width).wait_recv()
-        for sub in range(0, width, 256):
-            half_norms(CROSS, start + sub, 256)
-        own_cross(start, width, m)
-
-    @pl.loop(0, N_BIG)
-    def _(j):
-        start = mul(j, BIG)
-        arrive(j, start, BIG, 512)
-
-        @pl.loop(0, j)
-        def _(i):
-            far_tile(mul(i, BIG), BIG, start, BIG)
-
-        @pl.loop(0, j + 1)
-        def _(i):
-            far_tile(start, BIG, mul(i, BIG), BIG)
-
-    @pl.loop(0, N_SMALL)
-    def _(j):
-        start = pl.multiple_of(N_BIG * BIG + j * SMALL, SMALL)
-        arrive(N_BIG + j, start, SMALL, 1024)
-
-        @pl.loop(0, N_BIG)
-        def _(i):
-            far_tile(mul(i, BIG), BIG, start, SMALL)
-
-        @pl.loop(0, N_BIG)
-        def _(i):
-            far_tile(start, SMALL, mul(i, BIG), BIG)
-
-    far_tile(N_BIG * BIG, N_SMALL * SMALL, N_BIG * BIG, N_SMALL * SMALL)
+    def stage(j, pend):
+        start = mul(j, T)
+        x_copy(0, j, start, T).wait_recv()
+        forward(j, start, T).start()
+        x_copy(1, j, start, T).wait_recv()
+        half_norms(PLUS, start, T)
+        half_norms(MINUS, start, T)
+        pend = tiles(side, lambda i: (i, j), pend, OWN, PLUS, 2, OWN, PLUS, PLUS, OWN, True, 4)
+        forward(j, start, T).wait_recv()
+        half_norms(CROSS, start, T)
+        pend = tiles(side, lambda i: (i, j), pend, OWN, CROSS, 3, OWN, CROSS, CROSS, OWN, True, 4)
+        pend = tiles(1, lambda i: (j, j), pend, PLUS, far, 4, PLUS, far, far, PLUS)
+        return tiles(2 * j, lambda i: (jnp.where(i % 2 == 0, i // 2, j), jnp.where(i % 2 == 0, j, i // 2)), pend,
+                     PLUS, far, 4, PLUS, far, far, PLUS, True, 2)
+
+    pend = lax.fori_loop(0, side, stage, nothing)
+    flush(pend, True)
 
     def exchange(step):
         to_plus, to_minus, to_sib = part_copies(step)
@@ -275,7 +258,7 @@
                 pltpu.VMEM((5, cols, rows), BF16),
                 pltpu.VMEM((5, cols, rows), BF16),
                 pltpu.VMEM((4, 1, rows), F32),
-                pltpu.VMEM((4, cols, rows), F32),
+                pltpu.VMEM((5, cols, rows), F32),
                 pltpu.VMEM((3, cols, rows), F32),
                 dma((2, N_PIECE)), dma((2, N_PIECE)), dma((N_PIECE,)), dma((N_PIECE,)),
                 dma, dma, dma((2,)), dma((4,)), dma((4,)), dma((4,)), dma((4,)),

time: 147 us -> 139 us (0.946)
  Pallas kernels: 143 us -> 135 us
    pallas_call x1, Pallas kernels: 143 us -> 135 us  [local_program(): pl.pallas_call(functools.partial(kernel, n_row), out_shape=jax.ShapeDtype...]
where the time goes in v2:
time: 139 us
  Pallas kernels  135 us (97%)
  local copies, waits for them, and re-layouts  1.87 us (1%)
    pallas_call x1, Pallas kernels, local_program(): pl.pallas_call(functools.partial(kernel, n_row), out_shape=jax.ShapeDtype...  135 us

profile of v2, /device:TPU:112, one launch (start us, length us, event | category | flops | bytes accessed | tf_op | source)
XLA Modules:
  0.0 138.9 jit_solution(3058541532753680601)
XLA Ops:
  1.3 0.6 maximum_bitcast_fusion.coef
  1.9 135.1 %shard_map.46 = f32[64,2048]{1,0:T(8,128)} custom-call(bf16[2048,768]{1,0:T(8,128)(2,1)} %x_hbm.1, bf16[64,2048]{1,0:T(8,128)(2,1)} %bitcast.5, f32[1,2]{1,0:T(1,128)} %maximum_bitcast_fusion.coef), custom_call_target="tpu_custom_call" | custom-call | tf_op jit(solution)/shard_map/pallas_call | solution.py:249
  137.0 1.9 %copy.8 = f32[2048,64]{0,1:T(8,128)} copy(f32[2048,64]{0,1:T(8,128)} %bitcast.4) | data formatting | bytes 1048576

commit v3 on v2

--- a/solution.py
+++ b/solution.py
@@ -24,7 +24,7 @@
     return lax.dot_general(a, b, (((1,), (1,)), ((), ())), preferred_element_type=F32)
 
 
-def kernel(n_row, x_hbm, vt_hbm, coef, out_hbm, xb, kb, vb, yb, hr, acc, rb,
+def kernel(n_row, x_hbm, vt_hbm, coef, out_hbm, xb, kb, vb, yb, hr, acc, acc2, rb,
            x_s, x_r, f_s, f_r, sib_s, sib_r, loc, v_s, v_r, y_s, y_r, p_s, p_r, free):
     rows = xb.shape[1]
     me = lax.axis_index("row")
@@ -48,16 +48,23 @@
         return remote(xb.at[MINUS, pl.ds(start, width)], xb.at[CROSS, pl.ds(start, width)],
                       f_s.at[piece], f_r.at[piece], sib)
 
-    def vec_copies(src, buf, s_sem, r_sem):
-        return (remote(src, buf.at[MINUS], s_sem.at[0], r_sem.at[0], plus),
-                remote(src, buf.at[PLUS], s_sem.at[1], r_sem.at[1], minus),
-                remote(src, buf.at[SIB], s_sem.at[2], r_sem.at[2], sib),
-                remote(buf.at[MINUS], buf.at[CROSS], s_sem.at[3], r_sem.at[3], sib))
-
-    def part_copies(step):
-        return (remote(acc.at[PLUS], rb.at[0], p_s.at[step, 0], p_r.at[step, 0], plus),
-                remote(acc.at[MINUS], rb.at[1], p_s.at[step, 1], p_r.at[step, 1], minus),
-                remote(acc.at[CROSS], rb.at[2], p_s.at[step, 2], p_r.at[step, 2], sib))
+    def vec_copies(own, src, buf, s_sem, r_sem):
+        return (remote(own, src(buf, MINUS), s_sem(0), r_sem(0), plus),
+                remote(own, src(buf, PLUS), s_sem(1), r_sem(1), minus),
+                remote(own, src(buf, SIB), s_sem(2), r_sem(2), sib),
+                remote(src(buf, MINUS), src(buf, CROSS), s_sem(3), r_sem(3), sib))
+
+    def y_copies(k):
+        part = lambda buf, slot: buf.at[slot, :, pl.ds(mul(k, T), T)]
+        return vec_copies(part(yb, OWN), part, yb, lambda d: y_s.at[d, k], lambda d: y_r.at[d, k])
+
+    def part_copies(step, buf, k):
+        cols = pl.ds(mul(k, T), T)
+        return tuple(remote(buf.at[slot, :, cols], rb.at[i, :, cols], p_s.at[step, i, k], p_r.at[step, i, k], dev)
+                     for i, (slot, dev) in enumerate(((PLUS, plus), (MINUS, minus), (CROSS, sib))))
+
+    def mul(i, size):
+        return i * size if isinstance(i, int) else pl.multiple_of(i * size, size)
 
     pieces = [(i, i * T, T) for i in range(N_PIECE)]
 
@@ -70,7 +77,8 @@
     own_v = pltpu.make_async_copy(vt_hbm, vb.at[OWN], loc.at[1])
     own_x.start()
     own_v.start()
-    v_plus, v_minus, v_sib, v_cross = vec_copies(vt_hbm, vb, v_s, v_r)
+    v_plus, v_minus, v_sib, v_cross = vec_copies(
+        vt_hbm, lambda buf, slot: buf.at[slot], vb, lambda d: v_s.at[d], lambda d: v_r.at[d])
     sib_x = remote(x_hbm, xb.at[CROSS], sib_s, sib_r, sib)
     v_plus.start()
     v_minus.start()
@@ -127,10 +135,8 @@
 
     nothing = tuple(jnp.int32(v) for v in (0, 0, 0, OWN, TRASH, OWN, TRASH))
 
-    def mul(i, size):
-        return pl.multiple_of(i * size, size)
-
     acc[...] = jnp.zeros_like(acc)
+    acc2[...] = jnp.zeros_like(acc2)
     own_x.wait()
     own_v.wait()
 
@@ -174,67 +180,87 @@
     pend = lax.fori_loop(0, side, stage, nothing)
     flush(pend, True)
 
-    def exchange(step):
-        to_plus, to_minus, to_sib = part_copies(step)
-        to_sib.start()
-        to_plus.start()
-        to_sib.wait_recv()
-        acc[MINUS] += rb[2]
-        to_minus.start()
-        return to_plus, to_minus, to_sib
-
-    copies = exchange(0)
-    copies[0].wait_recv()
-    copies[1].wait_recv()
-    yb[OWN] = (acc[OWN] + rb[0] + rb[1]).astype(BF16)
-    y_plus, y_minus, y_sib, y_cross = vec_copies(yb.at[OWN], yb, y_s, y_r)
-    y_plus.start()
-    y_minus.start()
-    y_sib.start()
-    for copy in copies:
+    def exchange(step, buf):
+        for k in range(N_PIECE):
+            to_plus, _, to_sib = part_copies(step, buf, k)
+            to_sib.start()
+            to_plus.start()
+        for k in range(N_PIECE):
+            cols = pl.ds(k * T, T)
+            _, to_minus, to_sib = part_copies(step, buf, k)
+            to_sib.wait_recv()
+            buf[MINUS, :, cols] += rb[2, :, cols]
+            to_minus.start()
+
+    def arrived(step, buf, k):
+        to_plus, to_minus, _ = part_copies(step, buf, k)
+        to_plus.wait_recv()
+        to_minus.wait_recv()
+
+    def apply_nn(k_slot, y_slot, out, k):
+        piece = pl.ds(mul(k, T), T)
+        acc2[out] += dot_nn(yb[y_slot, :, piece], kb[k_slot, piece, :])
+
+    def apply_nt(k_slot, y_slot, out, k):
+        piece = pl.ds(mul(k, T), T)
+        acc2[out] += dot_nt(yb[y_slot, :, piece], kb[k_slot, :, piece])
+
+    exchange(0, acc)
+
+    @pl.loop(0, N_PIECE)
+    def _(k):
+        piece = pl.ds(mul(k, T), T)
+        arrived(0, acc, k)
+        yb[OWN, :, piece] = (acc[OWN, :, piece] + rb[0, :, piece] + rb[1, :, piece]).astype(BF16)
+        y_plus, y_minus, y_sib, _ = y_copies(k)
+        y_plus.start()
+        y_minus.start()
+        y_sib.start()
+        apply_nn(2, OWN, PLUS, k)
+        apply_nn(3, OWN, CROSS, k)
+        apply_nn(0, OWN, OWN, k)
+
+    @pl.loop(0, N_PIECE)
+    def _(k):
+        y_plus, y_minus, y_sib, y_cross = y_copies(k)
+        y_sib.wait_recv()
+        apply_nn(1, SIB, OWN, k)
+
+    @pl.loop(0, N_PIECE)
+    def _(k):
+        y_plus, y_minus, y_sib, y_cross = y_copies(k)
+        y_plus.wait_recv()
+        y_cross.start()
+        y_minus.wait_recv()
+        apply_nn(4, PLUS, far, k)
+        y_cross.wait_recv()
+        apply_nt(4, far, PLUS, k)
+
+    exchange(1, acc2)
+
+    @pl.loop(0, N_PIECE)
+    def _(k):
+        apply_nt(2, PLUS, OWN, k)
+        apply_nt(3, CROSS, OWN, k)
+
+    def out_copy(k):
+        piece = pl.ds(k * T, T)
+        return pltpu.make_async_copy(acc.at[OWN, :, piece], out_hbm.at[:, piece], loc.at[k])
+
+    for k in range(N_PIECE):
+        piece = pl.ds(k * T, T)
+        arrived(1, acc2, k)
+        acc[OWN, :, piece] = acc2[OWN, :, piece] + rb[0, :, piece] + rb[1, :, piece]
+        out_copy(k).start()
+    for copy in (v_plus, v_minus, v_sib, v_cross, sib_x):
         copy.wait_send()
-    acc[...] = jnp.zeros_like(acc)
-
-    half = rows // 2
-
-    def apply_nn(k_slot, y_slot, out):
-        for q0 in (0, half):
-            acc[out, :, pl.ds(q0, half)] += dot_nn(yb[y_slot], kb[k_slot, :, pl.ds(q0, half)])
-
-    def apply_nt(k_slot, y_slot, out):
-        for p0 in (0, half):
-            acc[out, :, pl.ds(p0, half)] += dot_nt(yb[y_slot], kb[k_slot, pl.ds(p0, half), :])
-
-    @pl.loop(0, 3)
-    def _(i):
-        apply_nn((2 + i) % 4, OWN, (1 + 2 * i) % 5)
-
-    y_sib.wait_recv()
-    apply_nn(1, SIB, OWN)
-    y_plus.wait_recv()
-    y_cross.start()
-    y_minus.wait_recv()
-    apply_nn(4, PLUS, far)
-    y_cross.wait_recv()
-    apply_nt(4, far, PLUS)
-    to_plus, to_minus, to_sib = exchange(1)
-
-    @pl.loop(0, 2)
-    def _(i):
-        apply_nt(2 + i, 1 + 2 * i, OWN)
-
-    to_plus.wait_recv()
-    to_minus.wait_recv()
-    acc[OWN] += rb[0] + rb[1]
-    out_copy = pltpu.make_async_copy(acc.at[OWN], out_hbm, loc.at[0])
-    out_copy.start()
-    for copy in (to_plus, to_minus, to_sib, y_plus, y_minus, y_sib, y_cross, v_plus, v_minus, v_sib, v_cross, sib_x):
-        copy.wait_send()
-    for piece in pieces:
-        x_copy(0, *piece).wait_send()
-        x_copy(1, *piece).wait_send()
-        forward(*piece).wait_send()
-    out_copy.wait()
+    for k in range(N_PIECE):
+        for copy in part_copies(0, acc, k) + part_copies(1, acc2, k) + y_copies(k):
+            copy.wait_send()
+        x_copy(0, *pieces[k]).wait_send()
+        x_copy(1, *pieces[k]).wait_send()
+        forward(*pieces[k]).wait_send()
+        out_copy(k).wait()
 
 
 def solution(mesh):
@@ -259,10 +285,11 @@
                 pltpu.VMEM((5, cols, rows), BF16),
                 pltpu.VMEM((4, 1, rows), F32),
                 pltpu.VMEM((5, cols, rows), F32),
+                pltpu.VMEM((4, cols, rows), F32),
                 pltpu.VMEM((3, cols, rows), F32),
                 dma((2, N_PIECE)), dma((2, N_PIECE)), dma((N_PIECE,)), dma((N_PIECE,)),
-                dma, dma, dma((2,)), dma((4,)), dma((4,)), dma((4,)), dma((4,)),
-                dma((2, 3)), dma((2, 3)), pltpu.SemaphoreType.REGULAR,
+                dma, dma, dma((N_PIECE,)), dma((4,)), dma((4,)), dma((4, N_PIECE)), dma((4, N_PIECE)),
+                dma((2, 3, N_PIECE)), dma((2, 3, N_PIECE)), pltpu.SemaphoreType.REGULAR,
             ],
             compiler_params=pltpu.CompilerParams(
                 collective_id=0, has_side_effects=True, vmem_limit_bytes=67043328),

time: 139 us -> 137 us (0.986)
  Pallas kernels: 135 us -> 133 us
    pallas_call x1, Pallas kernels: 135 us -> 133 us  [local_program(): pl.pallas_call(functools.partial(kernel, n_row), out_shape=jax.ShapeDtype...]
where the time goes in v3:
time: 137 us
  Pallas kernels  133 us (97%)
  local copies, waits for them, and re-layouts  1.87 us (1%)
    pallas_call x1, Pallas kernels, local_program(): pl.pallas_call(functools.partial(kernel, n_row), out_shape=jax.ShapeDtype...  133 us

profile of v3, /device:TPU:112, one launch (start us, length us, event | category | flops | bytes accessed | tf_op | source)
XLA Modules:
  0.0 136.6 jit_solution(10194058637681797391)
XLA Ops:
  1.3 0.6 maximum_bitcast_fusion.coef
  1.9 132.8 %shard_map.46 = f32[64,2048]{1,0:T(8,128)} custom-call(bf16[2048,768]{1,0:T(8,128)(2,1)} %x_hbm.1, bf16[64,2048]{1,0:T(8,128)(2,1)} %bitcast.5, f32[1,2]{1,0:T(1,128)} %maximum_bitcast_fusion.coef), custom_call_target="tpu_custom_call" | custom-call | tf_op jit(solution)/shard_map/pallas_call | solution.py:275
  134.7 1.9 %copy.8 = f32[2048,64]{0,1:T(8,128)} copy(f32[2048,64]{0,1:T(8,128)} %bitcast.4) | data formatting | bytes 1048576

commit v4 on v3

v4 whole, which is shorter than its diff:
```python
import functools

import jax
import jax.numpy as jnp
from jax import lax
from jax.experimental import pallas as pl
from jax.experimental.pallas import tpu as pltpu
from jax.sharding import PartitionSpec as P

F32 = jnp.float32
BF16 = jnp.bfloat16
LOG2E = 1.4426950408889634
OWN, PLUS, MINUS, CROSS, SIB = 0, 1, 2, 3, 4
N_SUM = 4
TRASH = 7
T = 512
N_PIECE = 4


def dot_nn(a, b):
    return lax.dot_general(a, b, (((1,), (0,)), ((), ())), preferred_element_type=F32)


def dot_nt(a, b):
    return lax.dot_general(a, b, (((1,), (1,)), ((), ())), preferred_element_type=F32)


def kernel(n_row, x_hbm, vt_hbm, length_scale, out_scale, out_hbm, xb, kb, vb, yb, hr, acc, rb,
           x_s, x_r, f_s, f_r, sib_s, sib_r, loc, v_s, v_r, y_s, y_r, p_s, p_r, free):
    rows = xb.shape[1]
    me = lax.axis_index("row")
    core = me % 2
    sib = me + 1 - 2 * core
    plus = (me + 2) % n_row
    minus = (me + n_row - 2) % n_row
    half_ring = n_row // 2

    def order(dev, j):
        flip = dev // half_ring
        return j + flip * (N_PIECE - 1 - 2 * j)

    def remote(src, dst, s_sem, r_sem, dev):
        return pltpu.make_async_remote_copy(
            src_ref=src, dst_ref=dst, send_sem=s_sem, recv_sem=r_sem,
            device_id={"row": dev}, device_id_type=pl.DeviceIdType.MESH)

    def x_send(direction, j):
        slot, dev = ((MINUS, plus), (PLUS, minus))[direction]
        piece = pl.ds(mul(order(dev, j), T), T)
        return remote(x_hbm.at[piece], xb.at[slot, piece], x_s.at[direction, j], x_r.at[direction, j], dev)

    def x_recv(direction, j):
        slot, dev = ((MINUS, plus), (PLUS, minus))[direction]
        piece = pl.ds(mul(order(me, j), T), T)
        return remote(x_hbm.at[piece], xb.at[slot, piece], x_s.at[direction, j], x_r.at[direction, j], dev)

    def forward(j):
        piece = pl.ds(mul(order(me, j), T), T)
        return remote(xb.at[MINUS, piece], xb.at[CROSS, piece], f_s.at[j], f_r.at[j], sib)

    def vec_copies(own, place, s_sem, r_sem):
        return (remote(own, place(MINUS), s_sem(0), r_sem(0), plus),
                remote(own, place(PLUS), s_sem(1), r_sem(1), minus),
                remote(own, place(SIB), s_sem(2), r_sem(2), sib),
                remote(place(MINUS), place(CROSS), s_sem(3), r_sem(3), sib))

    def y_ref(slot):
        return vb.at[slot] if slot in (OWN, SIB) else yb.at[slot - PLUS]

    def y_copies(k):
        piece = pl.ds(mul(k, T), T)
        return vec_copies(y_ref(OWN).at[:, piece], lambda slot: y_ref(slot).at[:, piece],
                          lambda d: y_s.at[d, k], lambda d: y_r.at[d, k])

    def part_copies(step, k):
        cols = pl.ds(mul(k, T), T)
        return tuple(remote(acc.at[step * N_SUM + slot, :, cols], rb.at[i, :, cols], p_s.at[step, i, k], p_r.at[step, i, k], dev)
                     for i, (slot, dev) in enumerate(((PLUS, plus), (MINUS, minus), (CROSS, sib))))

    def mul(i, size):
        return i * size if isinstance(i, int) else pl.multiple_of(i * size, size)

    barrier = pltpu.get_barrier_semaphore()
    for dev in (sib, plus, minus):
        pl.semaphore_signal(barrier, inc=1, device_id={"row": dev}, device_id_type=pl.DeviceIdType.MESH)
    pl.semaphore_wait(barrier, 3)

    own_x = pltpu.make_async_copy(x_hbm, xb.at[OWN], loc.at[0])
    own_v = pltpu.make_async_copy(vt_hbm, vb.at[OWN], loc.at[1])
    own_x.start()
    own_v.start()
    v_plus, v_minus, v_sib, v_cross = vec_copies(
        vt_hbm, lambda slot: vb.at[slot], lambda d: v_s.at[d], lambda d: v_r.at[d])
    sib_x = remote(x_hbm, xb.at[CROSS], sib_s, sib_r, sib)
    v_plus.start()
    v_minus.start()
    for j in range(N_PIECE):
        x_send(0, j).start()
        x_send(1, j).start()
    v_sib.start()
    sib_x.start()

    scale = jnp.full((8, 128), length_scale[0], F32)
    coef_d = (-LOG2E / (scale * scale))[0, 0]
    coef_s = out_scale[0]
    eye = (lax.broadcasted_iota(jnp.int32, (128, 128), 0) == lax.broadcasted_iota(jnp.int32, (128, 128), 1))

    def half_norms(slot, start, width):
        for sub in range(0, width, 128):
            x_sub = xb[slot, pl.ds(start + sub, 128), :].astype(F32)
            col = jnp.sum(x_sub * x_sub, axis=1, keepdims=True) * 0.5
            hr[slot, :, pl.ds(start + sub, 128)] = jnp.sum(jnp.where(eye, col, 0.0), axis=0, keepdims=True)

    def products(t, both):
        k_slot, k_row, k_col, p0, q0, v_p, v_q, acc_p, acc_q = t
        p_piece, q_piece = pl.ds(pl.multiple_of(p0, T), T), pl.ds(pl.multiple_of(q0, T), T)
        k_tile = kb[k_slot, pl.ds(pl.multiple_of(k_row, T), T), pl.ds(pl.multiple_of(k_col, T), T)]
        acc[acc_q, :, q_piece] += dot_nn(vb[v_p, :, p_piece], k_tile)
        if both:
            acc[acc_p, :, p_piece] += dot_nt(vb[v_q, :, q_piece], k_tile)

    def tile(p_slot, q_slot, t, pend, both):
        k_slot, k_row, k_col, p0, q0 = t[:5]
        k_row, k_col, p0, q0 = (pl.multiple_of(v, T) for v in (k_row, k_col, p0, q0))
        gram = dot_nt(xb[p_slot, pl.ds(p0, T), :], xb[q_slot, pl.ds(q0, T), :])
        products(pend, both)
        h_q = hr[q_slot, :, pl.ds(q0, T)]
        for sub in range(0, T, 128):
            h_row = hr[p_slot, :, pl.ds(p0 + sub, 128)]
            h_p = jnp.sum(jnp.where(eye, h_row, 0.0), axis=1, keepdims=True)
            half_d = jnp.maximum(h_p + h_q - gram[sub:sub + 128], 0.0)
            kb[k_slot, pl.ds(k_row + sub, 128), pl.ds(k_col, T)] = (coef_s * jnp.exp2(half_d * coef_d)).astype(BF16)

    def tiles(count, unroll, place, pend, both=True):
        def step(i, pend):
            for sub in range(unroll):
                p_slot, q_slot, t = place(i, sub)
                t = tuple(jnp.int32(v) for v in t)
                tile(p_slot, q_slot, t, pend, both)
                pend = t
            return pend

        return lax.fori_loop(0, count, step, pend)

    nothing = tuple(jnp.int32(v) for v in (0, 0, 0, 0, 0, OWN, OWN, TRASH, TRASH))

    acc[...] = jnp.zeros_like(acc)
    own_x.wait()
    own_v.wait()

    def norm_loop(slot):
        @pl.loop(0, rows // 256)
        def _(i):
            half_norms(slot, mul(i, 256), 256)

    norm_loop(OWN)
    side = rows // T
    pend = tiles(side, side, lambda i, sub: (OWN, OWN, (0, i * T, sub * T, i * T, sub * T, OWN, OWN, TRASH, OWN)), nothing, False)

    sib_x.wait_recv()
    v_sib.wait_recv()
    norm_loop(CROSS)

    pend = tiles(side, side, lambda i, sub: (CROSS, OWN, (1, i * T, sub * T, i * T, sub * T, SIB, OWN, TRASH, OWN)), pend, False)
    products(pend, False)
    pl.semaphore_signal(free, inc=1, device_id={"row": sib}, device_id_type=pl.DeviceIdType.MESH)
    v_minus.wait_recv()
    v_plus.wait_recv()
    v_cross.start()
    pl.semaphore_wait(free, 1)
    v_cross.wait_recv()

    def own_tiles(slot, j, pend):
        q0 = order(me, j) * T
        k_slot = 2 if slot == PLUS else 3
        return tiles(1, side, lambda i, sub: (OWN, slot, (k_slot, sub * T, q0, sub * T, q0, OWN, slot, OWN, slot)), pend)

    swap = me // half_ring

    def far_slots(which):
        other = MINUS + which
        return PLUS + swap * (other - PLUS), other + swap * (PLUS - other)

    def far_place(r, q, which):
        k_row = r + which * (N_PIECE - 1 - 2 * r)
        k_col = q + which * (N_PIECE - 1 - 2 * q)
        return k_row * T, k_col * T, order(me, r) * T, order(me, q) * T

    def far_tiles(count, j, pend):
        def place(i, which):
            r = jnp.where(i == 0, 0, jnp.where(i == 1, j, 1))
            q = jnp.where(i == 1, 0, j)
            p_slot, q_slot = far_slots(which)
            return p_slot, q_slot, (4,) + far_place(r, q, which) + (p_slot, q_slot, p_slot, q_slot)

        return tiles(count, 2, place, pend)

    def arrive(j):
        start = mul(order(me, j), T)
        x_recv(0, j).wait_recv()
        forward(j).start()
        x_recv(1, j).wait_recv()
        half_norms(PLUS, start, T)
        half_norms(MINUS, start, T)

    def arrive_cross(j):
        forward(j).wait_recv()
        half_norms(CROSS, mul(order(me, j), T), T)

    def stage(j, pend):
        arrive(j)
        pend = own_tiles(PLUS, j, pend)
        arrive_cross(j)
        pend = own_tiles(CROSS, j, pend)
        return far_tiles(jnp.where(j == 0, 1, 3), j, pend)

    def to_plus(step, j):
        return part_copies(step, order(me, j))[0]

    def to_minus(step, j):
        return part_copies(step, order(me, j))[1]

    def to_sib(step, j):
        return part_copies(step, order(me, j))[2]

    def combine(step, j):
        piece = pl.ds(mul(order(me, j), T), T)
        to_sib(step, j).wait_recv()
        acc[step * N_SUM + MINUS, :, piece] += rb[2, :, piece]
        to_minus(step, j).start()

    def arrived(step, k):
        for copy in part_copies(step, k)[:2]:
            copy.wait_recv()

    pend = lax.fori_loop(0, side - 1, stage, nothing)
    products(pend, True)
    for j in (1, 2):
        to_sib(0, j).start()
        to_plus(0, j).start()
    for j in (1, 2):
        combine(0, j)
    last = side - 1
    arrive(last)
    arrive_cross(last)
    pend = far_tiles(1, last, nothing)
    pend = own_tiles(CROSS, last, pend)
    to_sib(0, 0).start()
    to_plus(0, 0).start()
    pend = own_tiles(PLUS, last, pend)
    to_sib(0, last).start()
    combine(0, 0)
    products(pend, True)
    to_plus(0, last).start()
    combine(0, last)
    acc[pl.ds(N_SUM, N_SUM)] = jnp.zeros((N_SUM,) + acc.shape[1:], F32)

    def apply_nn(k_slot, y_slot, out, k):
        piece = pl.ds(mul(k, T), T)
        acc[N_SUM + out] += dot_nn(y_ref(y_slot)[:, piece], kb[k_slot, piece, :])

    def apply_nt(k_slot, y_slot, out, k):
        piece = pl.ds(mul(k, T), T)
        acc[N_SUM + out] += dot_nt(y_ref(y_slot)[:, piece], kb[k_slot, :, piece])

    def make_y(k):
        piece = pl.ds(mul(k, T), T)
        arrived(0, k)
        y_ref(OWN)[:, piece] = (acc[OWN, :, piece] + rb[0, :, piece] + rb[1, :, piece]).astype(BF16)

    def apply_own(k):
        apply_nn(2, OWN, PLUS, k)
        apply_nn(3, OWN, CROSS, k)
        apply_nn(0, OWN, OWN, k)

    @pl.loop(1, 3)
    def _(k):
        make_y(k)
        y_plus, y_minus, y_sib, _ = y_copies(k)
        y_plus.start()
        y_minus.start()
        y_sib.start()
        apply_own(k)

    first, final = order(minus, 0), order(minus, N_PIECE - 1)
    make_y(first)
    make_y(final)
    y_copies(first)[1].start()
    y_copies(final)[0].start()
    y_copies(final)[1].start()
    y_copies(first)[0].start()
    y_copies(first)[2].start()
    y_copies(final)[2].start()

    @pl.loop(0, 2)
    def _(i):
        apply_own(first + i * (final - first))


    @pl.loop(0, N_PIECE)
    def _(k):
        y_copies(k)[2].wait_recv()
        apply_nn(1, SIB, OWN, k)

    def far_products(group):
        for which in (0, 1):
            p_slot, q_slot = far_slots(which)

            def y_piece(slot, start):
                return yb[slot - PLUS, :, pl.ds(pl.multiple_of(start, T), T)]

            for q in sorted({q for _, q in group}):
                total = None
                for r in sorted({r for r, c in group if c == q}):
                    k_row, k_col, p0, q0 = far_place(r, q, which)
                    part = dot_nn(y_piece(p_slot, p0), kb[4, k_row:k_row + T, k_col:k_col + T])
                    total = part if total is None else total + part
                acc[N_SUM + q_slot, :, pl.ds(pl.multiple_of(q0, T), T)] += total
            for r in sorted({r for r, _ in group}):
                total = None
                for q in sorted({q for c, q in group if c == r}):
                    k_row, k_col, p0, q0 = far_place(r, q, which)
                    part = dot_nt(y_piece(q_slot, q0), kb[4, k_row:k_row + T, k_col:k_col + T])
                    total = part if total is None else total + part
                acc[N_SUM + p_slot, :, pl.ds(pl.multiple_of(p0, T), T)] += total

    def y_arrive(js):
        for j in js:
            y_copies(order(me, j))[0].wait_recv()
            y_copies(order(me, j))[3].start()
        for j in js:
            y_copies(order(me, j))[1].wait_recv()
            y_copies(order(me, j))[3].wait_recv()

    y_arrive((1, 2))
    far_products(((1, 1), (1, 2)))
    y_arrive((0,))
    far_products(((0, 0), (0, 1), (1, 0), (0, 2), (2, 0)))
    for j in (1, 2):
        to_sib(1, j).start()
        to_plus(1, j).start()
    for j in (1, 2):
        combine(1, j)
    y_arrive((last,))
    far_products(((0, last),))
    for j in (0, last):
        to_sib(1, j).start()
        to_plus(1, j).start()
    for j in (0, last):
        combine(1, j)

    @pl.loop(0, N_PIECE)
    def _(k):
        apply_nt(2, PLUS, OWN, k)
        apply_nt(3, CROSS, OWN, k)

    def out_copy(k):
        piece = pl.ds(mul(k, T), T)
        return pltpu.make_async_copy(acc.at[OWN, :, piece], out_hbm.at[:, piece], loc.at[k])

    for k in (1, 2, first, final):
        piece = pl.ds(mul(k, T), T)
        arrived(1, k)
        acc[OWN, :, piece] = acc[N_SUM + OWN, :, piece] + rb[0, :, piece] + rb[1, :, piece]
        out_copy(k).start()
    for copy in (v_plus, v_minus, v_sib, v_cross, sib_x):
        copy.wait_send()
    for k in range(N_PIECE):
        for copy in part_copies(0, k) + part_copies(1, k) + y_copies(k):
            copy.wait_send()
        x_send(0, k).wait_send()
        x_send(1, k).wait_send()
        forward(k).wait_send()
        out_copy(k).wait()


def solution(mesh):
    n_row = mesh.shape["row"]
    assert n_row == 8

    def local_program(x_loc, v_loc, length_scale, out_scale):
        rows, feat = x_loc.shape
        cols = v_loc.shape[1]
        dma = pltpu.SemaphoreType.DMA
        out = pl.pallas_call(
            functools.partial(kernel, n_row),
            out_shape=jax.ShapeDtypeStruct((cols, rows), F32),
            in_specs=[pl.BlockSpec(memory_space=pl.ANY), pl.BlockSpec(memory_space=pl.ANY),
                      pl.BlockSpec(memory_space=pltpu.SMEM), pl.BlockSpec(memory_space=pltpu.SMEM)],
            out_specs=pl.BlockSpec(memory_space=pl.ANY),
            scratch_shapes=[
                pltpu.VMEM((4, rows, feat), BF16),
                pltpu.VMEM((5, rows, rows), BF16),
                pltpu.VMEM((5, cols, rows), BF16),
                pltpu.VMEM((3, cols, rows), BF16),
                pltpu.VMEM((4, 1, rows), F32),
                pltpu.VMEM((2 * N_SUM, cols, rows), F32),
                pltpu.VMEM((3, cols, rows), F32),
                dma((2, N_PIECE)), dma((2, N_PIECE)), dma((N_PIECE,)), dma((N_PIECE,)),
                dma, dma, dma((N_PIECE,)), dma((4,)), dma((4,)), dma((4, N_PIECE)), dma((4, N_PIECE)),
                dma((2, 3, N_PIECE)), dma((2, 3, N_PIECE)), pltpu.SemaphoreType.REGULAR,
            ],
            compiler_params=pltpu.CompilerParams(
                collective_id=0, has_side_effects=True, vmem_limit_bytes=67043328),
        )(x_loc, v_loc.T, length_scale, out_scale)
        return out.T

    row_spec = P(("task", "row"), None)
    return jax.shard_map(local_program, mesh=mesh, in_specs=(row_spec, row_spec, P("task"), P("task")),
                         out_specs=row_spec, check_vma=False)
```

time: 137 us -> 126 us (0.920)
  Pallas kernels: 133 us -> 123 us
    pallas_call x1, Pallas kernels: 133 us -> 123 us  [local_program(): pl.pallas_call(functools.partial(kernel, n_row), out_shape=jax.ShapeDtype...]
where the time goes in v4:
time: 126 us
  Pallas kernels  123 us (98%)
  local copies, waits for them, and re-layouts  1.87 us (1%)
  between operations  1.31 us (1%)
    pallas_call x1, Pallas kernels, local_program(): pl.pallas_call(functools.partial(kernel, n_row), out_shape=jax.ShapeDtype...  123 us

profile of v4, /device:TPU:112, one launch (start us, length us, event | category | flops | bytes accessed | tf_op | source)
XLA Modules:
  0.0 126.0 jit_solution(9327325636965767156)
XLA Ops:
  1.3 122.8 %shard_map.46 = f32[64,2048]{1,0:T(8,128)} custom-call(bf16[2048,768]{1,0:T(8,128)(2,1)} %x_hbm.1, bf16[64,2048]{1,0:T(8,128)(2,1)} %bitcast.3, f32[1]{0:T(128)S(6)} %copy.6.length_scale, f32[1]{0:T(128)S(6)} %copy.7.out_scale), custom_call_target="tpu_custom_call" | custom-call | tf_op jit(solution)/shard_map/pallas_call | solution.py:385
  124.1 1.9 %copy.8 = f32[2048,64]{0,1:T(8,128)} copy(f32[2048,64]{0,1:T(8,128)} %bitcast.2) | data formatting | bytes 1048576

commit v5 on v4

--- a/solution.py
+++ b/solution.py
@@ -115,15 +115,26 @@
         k_slot, k_row, k_col, p0, q0, v_p, v_q, acc_p, acc_q = t
         p_piece, q_piece = pl.ds(pl.multiple_of(p0, T), T), pl.ds(pl.multiple_of(q0, T), T)
         k_tile = kb[k_slot, pl.ds(pl.multiple_of(k_row, T), T), pl.ds(pl.multiple_of(k_col, T), T)]
+        yield
         acc[acc_q, :, q_piece] += dot_nn(vb[v_p, :, p_piece], k_tile)
+        yield
         if both:
             acc[acc_p, :, p_piece] += dot_nt(vb[v_q, :, q_piece], k_tile)
+        yield
+
+    def flush(pend, both):
+        for _ in products(pend, both):
+            pass
 
     def tile(p_slot, q_slot, t, pend, both):
         k_slot, k_row, k_col, p0, q0 = t[:5]
         k_row, k_col, p0, q0 = (pl.multiple_of(v, T) for v in (k_row, k_col, p0, q0))
-        gram = dot_nt(xb[p_slot, pl.ds(p0, T), :], xb[q_slot, pl.ds(q0, T), :])
-        products(pend, both)
+        pending = products(pend, both)
+        gram = None
+        for f in range(0, xb.shape[2], 256):
+            part = dot_nt(xb[p_slot, pl.ds(p0, T), pl.ds(f, 256)], xb[q_slot, pl.ds(q0, T), pl.ds(f, 256)])
+            gram = part if gram is None else gram + part
+            next(pending)
         h_q = hr[q_slot, :, pl.ds(q0, T)]
         for sub in range(0, T, 128):
             h_row = hr[p_slot, :, pl.ds(p0 + sub, 128)]
@@ -162,7 +173,7 @@
     norm_loop(CROSS)
 
     pend = tiles(side, side, lambda i, sub: (CROSS, OWN, (1, i * T, sub * T, i * T, sub * T, SIB, OWN, TRASH, OWN)), pend, False)
-    products(pend, False)
+    flush(pend, False)
     pl.semaphore_signal(free, inc=1, device_id={"row": sib}, device_id_type=pl.DeviceIdType.MESH)
     v_minus.wait_recv()
     v_plus.wait_recv()
@@ -170,10 +181,15 @@
     pl.semaphore_wait(free, 1)
     v_cross.wait_recv()
 
-    def own_tiles(slot, j, pend):
+    def own_tiles(slot, j, pend, begin=0, end=side):
         q0 = order(me, j) * T
         k_slot = 2 if slot == PLUS else 3
-        return tiles(1, side, lambda i, sub: (OWN, slot, (k_slot, sub * T, q0, sub * T, q0, OWN, slot, OWN, slot)), pend)
+
+        def place(i, sub):
+            p0 = (begin + sub) * T
+            return OWN, slot, (k_slot, p0, q0, p0, q0, OWN, slot, OWN, slot)
+
+        return tiles(1, end - begin, place, pend)
 
     swap = me // half_ring
 
@@ -234,7 +250,7 @@
             copy.wait_recv()
 
     pend = lax.fori_loop(0, side - 1, stage, nothing)
-    products(pend, True)
+    flush(pend, True)
     for j in (1, 2):
         to_sib(0, j).start()
         to_plus(0, j).start()
@@ -242,15 +258,18 @@
         combine(0, j)
     last = side - 1
     arrive(last)
+    pend = own_tiles(PLUS, last, nothing, 0, side // 2)
     arrive_cross(last)
-    pend = far_tiles(1, last, nothing)
-    pend = own_tiles(CROSS, last, pend)
+    pend = far_tiles(1, last, pend)
+    flush(pend, True)
     to_sib(0, 0).start()
     to_plus(0, 0).start()
-    pend = own_tiles(PLUS, last, pend)
+    pend = own_tiles(CROSS, last, nothing)
+    flush(pend, True)
     to_sib(0, last).start()
     combine(0, 0)
-    products(pend, True)
+    pend = own_tiles(PLUS, last, nothing, side // 2)
+    flush(pend, True)
     to_plus(0, last).start()
     combine(0, last)
     acc[pl.ds(N_SUM, N_SUM)] = jnp.zeros((N_SUM,) + acc.shape[1:], F32)
@@ -302,23 +321,23 @@
         y_copies(k)[2].wait_recv()
         apply_nn(1, SIB, OWN, k)
 
-    def far_products(group):
+    def far_products(group_nn, group_nt):
         for which in (0, 1):
             p_slot, q_slot = far_slots(which)
 
             def y_piece(slot, start):
                 return yb[slot - PLUS, :, pl.ds(pl.multiple_of(start, T), T)]
 
-            for q in sorted({q for _, q in group}):
+            for q in sorted({q for _, q in group_nn}):
                 total = None
-                for r in sorted({r for r, c in group if c == q}):
+                for r in sorted({r for r, c in group_nn if c == q}):
                     k_row, k_col, p0, q0 = far_place(r, q, which)
                     part = dot_nn(y_piece(p_slot, p0), kb[4, k_row:k_row + T, k_col:k_col + T])
                     total = part if total is None else total + part
                 acc[N_SUM + q_slot, :, pl.ds(pl.multiple_of(q0, T), T)] += total
-            for r in sorted({r for r, _ in group}):
+            for r in sorted({r for r, _ in group_nt}):
                 total = None
-                for q in sorted({q for c, q in group if c == r}):
+                for q in sorted({q for c, q in group_nt if c == r}):
                     k_row, k_col, p0, q0 = far_place(r, q, which)
                     part = dot_nt(y_piece(q_slot, q0), kb[4, k_row:k_row + T, k_col:k_col + T])
                     total = part if total is None else total + part
@@ -333,23 +352,26 @@
             y_copies(order(me, j))[3].wait_recv()
 
     y_arrive((1, 2))
-    far_products(((1, 1), (1, 2)))
+    far_products(((1, 1), (1, 2)), ((1, 1), (1, 2)))
     y_arrive((0,))
-    far_products(((0, 0), (0, 1), (1, 0), (0, 2), (2, 0)))
+    far_products(((0, 1), (0, 2)), ((1, 0), (2, 0)))
     for j in (1, 2):
         to_sib(1, j).start()
         to_plus(1, j).start()
+    far_products(((0, 0), (1, 0), (2, 0)), ((0, 0), (0, 1), (0, 2)))
     for j in (1, 2):
         combine(1, j)
     y_arrive((last,))
-    far_products(((0, last),))
+    far_products(((0, last),), ((0, last),))
     for j in (0, last):
         to_sib(1, j).start()
         to_plus(1, j).start()
+    apply_nt(2, PLUS, OWN, 0)
+    apply_nt(3, CROSS, OWN, 0)
     for j in (0, last):
         combine(1, j)
 
-    @pl.loop(0, N_PIECE)
+    @pl.loop(1, N_PIECE)
     def _(k):
         apply_nt(2, PLUS, OWN, k)
         apply_nt(3, CROSS, OWN, k)

time: 126 us -> 123 us (0.976)
  Pallas kernels: 123 us -> 120 us
    pallas_call x1, Pallas kernels: 123 us -> 120 us  [local_program(): pl.pallas_call(functools.partial(kernel, n_row), out_shape=jax.ShapeDtype...]
where the time goes in v5:
time: 123 us
  Pallas kernels  120 us (98%)
  local copies, waits for them, and re-layouts  1.87 us (2%)
  between operations  1.31 us (1%)
    pallas_call x1, Pallas kernels, local_program(): pl.pallas_call(functools.partial(kernel, n_row), out_shape=jax.ShapeDtype...  120 us

profile of v5, /device:TPU:112, one launch (start us, length us, event | category | flops | bytes accessed | tf_op | source)
XLA Modules:
  0.0 122.9 jit_solution(488727348994714355)
XLA Ops:
  1.3 119.7 %shard_map.46 = f32[64,2048]{1,0:T(8,128)} custom-call(bf16[2048,768]{1,0:T(8,128)(2,1)} %x_hbm.1, bf16[64,2048]{1,0:T(8,128)(2,1)} %bitcast.3, f32[1]{0:T(128)S(6)} %copy.6.length_scale, f32[1]{0:T(128)S(6)} %copy.7.out_scale), custom_call_target="tpu_custom_call" | custom-call | tf_op jit(solution)/shard_map/pallas_call | solution.py:407
  121.0 1.9 %copy.8 = f32[2048,64]{0,1:T(8,128)} copy(f32[2048,64]{0,1:T(8,128)} %bitcast.2) | data formatting | bytes 1048576

commit v6 on v5

--- a/solution.py
+++ b/solution.py
@@ -181,7 +181,7 @@
     pl.semaphore_wait(free, 1)
     v_cross.wait_recv()
 
-    def own_tiles(slot, j, pend, begin=0, end=side):
+    def own_tiles(slot, j, pend, begin=0, end=side, both=True):
         q0 = order(me, j) * T
         k_slot = 2 if slot == PLUS else 3
 
@@ -189,7 +189,7 @@
             p0 = (begin + sub) * T
             return OWN, slot, (k_slot, p0, q0, p0, q0, OWN, slot, OWN, slot)
 
-        return tiles(1, end - begin, place, pend)
+        return tiles(1, end - begin, place, pend, both)
 
     swap = me // half_ring
 
@@ -258,20 +258,20 @@
         combine(0, j)
     last = side - 1
     arrive(last)
-    pend = own_tiles(PLUS, last, nothing, 0, side // 2)
+    flush(own_tiles(PLUS, last, nothing, 0, side // 2, False), False)
     arrive_cross(last)
-    pend = far_tiles(1, last, pend)
-    flush(pend, True)
+    flush(far_tiles(1, last, nothing), True)
     to_sib(0, 0).start()
     to_plus(0, 0).start()
-    pend = own_tiles(CROSS, last, nothing)
-    flush(pend, True)
+    flush(own_tiles(CROSS, last, nothing, 0, side, False), False)
     to_sib(0, last).start()
     combine(0, 0)
-    pend = own_tiles(PLUS, last, nothing, side // 2)
-    flush(pend, True)
+    flush(own_tiles(PLUS, last, nothing, side // 2, side, False), False)
     to_plus(0, last).start()
     combine(0, last)
+    last_piece = pl.ds(mul(order(me, last), T), T)
+    acc[OWN] += (dot_nt(vb[PLUS, :, last_piece], kb[2, :, last_piece])
+                 + dot_nt(vb[CROSS, :, last_piece], kb[3, :, last_piece]))
     acc[pl.ds(N_SUM, N_SUM)] = jnp.zeros((N_SUM,) + acc.shape[1:], F32)
 
     def apply_nn(k_slot, y_slot, out, k):
@@ -311,15 +311,32 @@
     y_copies(first)[2].start()
     y_copies(final)[2].start()
 
+    def y_forward(j):
+        y_copies(order(me, j))[0].wait_recv()
+        y_copies(order(me, j))[3].start()
+
+    def y_rest(j):
+        y_copies(order(me, j))[1].wait_recv()
+        y_copies(order(me, j))[3].wait_recv()
+
+    def apply_sib(k):
+        y_copies(k)[2].wait_recv()
+        apply_nn(1, SIB, OWN, k)
+
+    y_forward(1)
+    y_forward(2)
+
     @pl.loop(0, 2)
     def _(i):
         apply_own(first + i * (final - first))
 
-
-    @pl.loop(0, N_PIECE)
-    def _(k):
-        y_copies(k)[2].wait_recv()
-        apply_nn(1, SIB, OWN, k)
+    apply_sib(1)
+    apply_sib(2)
+    y_forward(0)
+
+    @pl.loop(0, 2)
+    def _(i):
+        apply_sib(first + i * (final - first))
 
     def far_products(group_nn, group_nt):
         for which in (0, 1):
@@ -343,17 +360,11 @@
                     total = part if total is None else total + part
                 acc[N_SUM + p_slot, :, pl.ds(pl.multiple_of(p0, T), T)] += total
 
-    def y_arrive(js):
-        for j in js:
-            y_copies(order(me, j))[0].wait_recv()
-            y_copies(order(me, j))[3].start()
-        for j in js:
-            y_copies(order(me, j))[1].wait_recv()
-            y_copies(order(me, j))[3].wait_recv()
-
-    y_arrive((1, 2))
+    y_rest(1)
+    y_rest(2)
     far_products(((1, 1), (1, 2)), ((1, 1), (1, 2)))
-    y_arrive((0,))
+    y_forward(last)
+    y_rest(0)
     far_products(((0, 1), (0, 2)), ((1, 0), (2, 0)))
     for j in (1, 2):
         to_sib(1, j).start()
@@ -361,7 +372,7 @@
     far_products(((0, 0), (1, 0), (2, 0)), ((0, 0), (0, 1), (0, 2)))
     for j in (1, 2):
         combine(1, j)
-    y_arrive((last,))
+    y_rest(last)
     far_products(((0, last),), ((0, last),))
     for j in (0, last):
         to_sib(1, j).start()

time: 123 us -> 122 us (level)
  no operation moved by 1% of the time
where the time goes in v6:
time: 122 us
  Pallas kernels  119 us (98%)
  local copies, waits for them, and re-layouts  1.87 us (2%)
  between operations  1.31 us (1%)
    pallas_call x1, Pallas kernels, local_program(): pl.pallas_call(functools.partial(kernel, n_row), out_shape=jax.ShapeDtype...  119 us

profile of v6, /device:TPU:112, one launch (start us, length us, event | category | flops | bytes accessed | tf_op | source)
XLA Modules:
  0.0 122.0 jit_solution(16145724066399360455)
XLA Ops:
  1.3 118.9 %shard_map.46 = f32[64,2048]{1,0:T(8,128)} custom-call(bf16[2048,768]{1,0:T(8,128)(2,1)} %x_hbm.1, bf16[64,2048]{1,0:T(8,128)(2,1)} %bitcast.3, f32[1]{0:T(128)S(6)} %copy.6.length_scale, f32[1]{0:T(128)S(6)} %copy.7.out_scale), custom_call_target="tpu_custom_call" | custom-call | tf_op jit(solution)/shard_map/pallas_call | solution.py:418
  120.2 1.9 %copy.8 = f32[2048,64]{0,1:T(8,128)} copy(f32[2048,64]{0,1:T(8,128)} %bitcast.2) | data formatting | bytes 1048576

commit v7 on v6

--- a/solution.py
+++ b/solution.py
@@ -181,15 +181,15 @@
     pl.semaphore_wait(free, 1)
     v_cross.wait_recv()
 
-    def own_tiles(slot, j, pend, begin=0, end=side, both=True):
-        q0 = order(me, j) * T
-        k_slot = 2 if slot == PLUS else 3
-
-        def place(i, sub):
-            p0 = (begin + sub) * T
-            return OWN, slot, (k_slot, p0, q0, p0, q0, OWN, slot, OWN, slot)
-
-        return tiles(1, end - begin, place, pend, both)
+    def own_place(slot, j, sub):
+        p0, q0 = sub * T, order(me, j) * T
+        return OWN, slot, (2 if slot == PLUS else 3, p0, q0, p0, q0, OWN, slot, OWN, slot)
+
+    final = order(minus, side - 1)
+    spare = order(me, side - 1)
+
+    def minus_place(j):
+        return OWN, MINUS, (2, j * T, spare * T, final * T, order(me, j) * T, OWN, MINUS, OWN, MINUS)
 
     swap = me // half_ring
 
@@ -225,9 +225,9 @@
 
     def stage(j, pend):
         arrive(j)
-        pend = own_tiles(PLUS, j, pend)
+        pend = tiles(1, side + 1, lambda i, sub: own_place(PLUS, j, sub) if sub < side else minus_place(j), pend)
         arrive_cross(j)
-        pend = own_tiles(CROSS, j, pend)
+        pend = tiles(1, side, lambda i, sub: own_place(CROSS, j, sub), pend)
         return far_tiles(jnp.where(j == 0, 1, 3), j, pend)
 
     def to_plus(step, j):
@@ -258,20 +258,20 @@
         combine(0, j)
     last = side - 1
     arrive(last)
-    flush(own_tiles(PLUS, last, nothing, 0, side // 2, False), False)
+    flush(tiles(1, 1, lambda i, sub: minus_place(last), nothing), True)
     arrive_cross(last)
     flush(far_tiles(1, last, nothing), True)
     to_sib(0, 0).start()
     to_plus(0, 0).start()
-    flush(own_tiles(CROSS, last, nothing, 0, side, False), False)
+    to_plus(0, last).start()
+    pend = tiles(1, side // 2, lambda i, sub: own_place(CROSS, last, sub), nothing, False)
+    combine(0, 0)
+    pend = tiles(1, side // 2, lambda i, sub: own_place(CROSS, last, side // 2 + sub), pend, False)
+    flush(pend, False)
     to_sib(0, last).start()
-    combine(0, 0)
-    flush(own_tiles(PLUS, last, nothing, side // 2, side, False), False)
-    to_plus(0, last).start()
+    last_piece = pl.ds(mul(order(me, last), T), T)
+    acc[OWN] += dot_nt(vb[CROSS, :, last_piece], kb[3, :, last_piece])
     combine(0, last)
-    last_piece = pl.ds(mul(order(me, last), T), T)
-    acc[OWN] += (dot_nt(vb[PLUS, :, last_piece], kb[2, :, last_piece])
-                 + dot_nt(vb[CROSS, :, last_piece], kb[3, :, last_piece]))
     acc[pl.ds(N_SUM, N_SUM)] = jnp.zeros((N_SUM,) + acc.shape[1:], F32)
 
     def apply_nn(k_slot, y_slot, out, k):
@@ -287,10 +287,12 @@
         arrived(0, k)
         y_ref(OWN)[:, piece] = (acc[OWN, :, piece] + rb[0, :, piece] + rb[1, :, piece]).astype(BF16)
 
+    plus_cols = pl.ds(mul(me // half_ring, T), rows - T)
+
     def apply_own(k):
-        apply_nn(2, OWN, PLUS, k)
+        piece = pl.ds(mul(k, T), T)
+        acc[N_SUM + PLUS, :, plus_cols] += dot_nn(y_ref(OWN)[:, piece], kb[2, piece, plus_cols])
         apply_nn(3, OWN, CROSS, k)
-        apply_nn(0, OWN, OWN, k)
 
     @pl.loop(1, 3)
     def _(k):
@@ -301,7 +303,7 @@
         y_sib.start()
         apply_own(k)
 
-    first, final = order(minus, 0), order(minus, N_PIECE - 1)
+    first = order(minus, 0)
     make_y(first)
     make_y(final)
     y_copies(first)[1].start()
@@ -330,13 +332,11 @@
     def _(i):
         apply_own(first + i * (final - first))
 
-    apply_sib(1)
-    apply_sib(2)
+    spare_cols = pl.ds(mul(spare, T), T)
+    for j in range(N_PIECE):
+        acc[N_SUM + MINUS, :, pl.ds(mul(order(me, j), T), T)] += dot_nn(
+            y_ref(OWN)[:, pl.ds(mul(final, T), T)], kb[2, j * T:(j + 1) * T, spare_cols])
     y_forward(0)
-
-    @pl.loop(0, 2)
-    def _(i):
-        apply_sib(first + i * (final - first))
 
     def far_products(group_nn, group_nt):
         for which in (0, 1):
@@ -377,15 +377,25 @@
     for j in (0, last):
         to_sib(1, j).start()
         to_plus(1, j).start()
-    apply_nt(2, PLUS, OWN, 0)
-    apply_nt(3, CROSS, OWN, 0)
+    apply_nn(0, OWN, OWN, 0)
+    apply_sib(0)
     for j in (0, last):
         combine(1, j)
 
     @pl.loop(1, N_PIECE)
     def _(k):
-        apply_nt(2, PLUS, OWN, k)
-        apply_nt(3, CROSS, OWN, k)
+        apply_nn(0, OWN, OWN, k)
+        apply_sib(k)
+
+    @pl.loop(0, N_PIECE - 1)
+    def _(j):
+        apply_nt(2, PLUS, OWN, order(me, j))
+        apply_nt(3, CROSS, OWN, order(me, j))
+
+    apply_nt(3, CROSS, OWN, spare)
+    acc[N_SUM + OWN, :, pl.ds(mul(final, T), T)] += sum(
+        dot_nt(yb[MINUS - PLUS, :, pl.ds(mul(order(me, j), T), T)], kb[2, j * T:(j + 1) * T, spare_cols])
+        for j in range(N_PIECE))
 
     def out_copy(k):
         piece = pl.ds(mul(k, T), T)

time: 122 us -> 119 us (0.975)
  Pallas kernels: 119 us -> 116 us
    pallas_call x1, Pallas kernels: 119 us -> 116 us  [local_program(): pl.pallas_call(functools.partial(kernel, n_row), out_shape=jax.ShapeDtype...]
where the time goes in v7:
time: 119 us
  Pallas kernels  116 us (97%)
  local copies, waits for them, and re-layouts  1.87 us (2%)
  between operations  1.31 us (1%)
    pallas_call x1, Pallas kernels, local_program(): pl.pallas_call(functools.partial(kernel, n_row), out_shape=jax.ShapeDtype...  116 us

profile of v7, /device:TPU:112, one launch (start us, length us, event | category | flops | bytes accessed | tf_op | source)
XLA Modules:
  0.0 118.8 jit_solution(330924389001252218)
XLA Ops:
  1.3 115.7 %shard_map.46 = f32[64,2048]{1,0:T(8,128)} custom-call(bf16[2048,768]{1,0:T(8,128)(2,1)} %x_hbm.1, bf16[64,2048]{1,0:T(8,128)(2,1)} %bitcast.3, f32[1]{0:T(128)S(6)} %copy.6.length_scale, f32[1]{0:T(128)S(6)} %copy.7.out_scale), custom_call_target="tpu_custom_call" | custom-call | tf_op jit(solution)/shard_map/pallas_call | solution.py:428
  117.0 1.9 %copy.8 = f32[2048,64]{0,1:T(8,128)} copy(f32[2048,64]{0,1:T(8,128)} %bitcast.2) | data formatting | bytes 1048576

commit v8 on v7

--- a/solution.py
+++ b/solution.py
@@ -87,8 +87,6 @@
 
     own_x = pltpu.make_async_copy(x_hbm, xb.at[OWN], loc.at[0])
     own_v = pltpu.make_async_copy(vt_hbm, vb.at[OWN], loc.at[1])
-    own_x.start()
-    own_v.start()
     v_plus, v_minus, v_sib, v_cross = vec_copies(
         vt_hbm, lambda slot: vb.at[slot], lambda d: v_s.at[d], lambda d: v_r.at[d])
     sib_x = remote(x_hbm, xb.at[CROSS], sib_s, sib_r, sib)
@@ -97,6 +95,8 @@
     for j in range(N_PIECE):
         x_send(0, j).start()
         x_send(1, j).start()
+    own_x.start()
+    own_v.start()
     v_sib.start()
     sib_x.start()
 
@@ -202,12 +202,15 @@
         k_col = q + which * (N_PIECE - 1 - 2 * q)
         return k_row * T, k_col * T, order(me, r) * T, order(me, q) * T
 
+    def far_tile(r, q, which):
+        p_slot, q_slot = far_slots(which)
+        return p_slot, q_slot, (4,) + far_place(r, q, which) + (p_slot, q_slot, p_slot, q_slot)
+
     def far_tiles(count, j, pend):
         def place(i, which):
             r = jnp.where(i == 0, 0, jnp.where(i == 1, j, 1))
             q = jnp.where(i == 1, 0, j)
-            p_slot, q_slot = far_slots(which)
-            return p_slot, q_slot, (4,) + far_place(r, q, which) + (p_slot, q_slot, p_slot, q_slot)
+            return far_tile(r, q, which)
 
         return tiles(count, 2, place, pend)
 
@@ -258,9 +261,9 @@
         combine(0, j)
     last = side - 1
     arrive(last)
-    flush(tiles(1, 1, lambda i, sub: minus_place(last), nothing), True)
+    flush(tiles(1, 2, lambda i, sub: far_tile(0, last, 0) if sub else minus_place(last), nothing), True)
     arrive_cross(last)
-    flush(far_tiles(1, last, nothing), True)
+    flush(tiles(1, 1, lambda i, sub: far_tile(0, last, 1), nothing), True)
     to_sib(0, 0).start()
     to_plus(0, 0).start()
     to_plus(0, last).start()
@@ -336,10 +339,8 @@
     for j in range(N_PIECE):
         acc[N_SUM + MINUS, :, pl.ds(mul(order(me, j), T), T)] += dot_nn(
             y_ref(OWN)[:, pl.ds(mul(final, T), T)], kb[2, j * T:(j + 1) * T, spare_cols])
-    y_forward(0)
-
-    def far_products(group_nn, group_nt):
-        for which in (0, 1):
+    def far_products(group_nn, group_nt, pairs=(0, 1)):
+        for which in pairs:
             p_slot, q_slot = far_slots(which)
 
             def y_piece(slot, start):
@@ -363,12 +364,15 @@
     y_rest(1)
     y_rest(2)
     far_products(((1, 1), (1, 2)), ((1, 1), (1, 2)))
-    y_forward(last)
-    y_rest(0)
-    far_products(((0, 1), (0, 2)), ((1, 0), (2, 0)))
+    y_forward(0)
+    y_copies(order(me, 0))[1].wait_recv()
+    far_products(((0, 1), (0, 2)), ((1, 0), (2, 0)), (0,))
+    y_copies(order(me, 0))[3].wait_recv()
+    far_products(((0, 1), (0, 2)), ((1, 0), (2, 0)), (1,))
     for j in (1, 2):
         to_sib(1, j).start()
         to_plus(1, j).start()
+    y_forward(last)
     far_products(((0, 0), (1, 0), (2, 0)), ((0, 0), (0, 1), (0, 2)))
     for j in (1, 2):
         combine(1, j)

time: 119 us -> 118 us (level)
  no operation moved by 1% of the time
where the time goes in v8:
time: 118 us
  Pallas kernels  115 us (97%)
  local copies, waits for them, and re-layouts  1.87 us (2%)
  between operations  1.31 us (1%)
    pallas_call x1, Pallas kernels, local_program(): pl.pallas_call(functools.partial(kernel, n_row), out_shape=jax.ShapeDtype...  115 us

profile of v8, /device:TPU:112, one launch (start us, length us, event | category | flops | bytes accessed | tf_op | source)
XLA Modules:
  0.0 117.9 jit_solution(10323536319632222734)
XLA Ops:
  1.3 114.7 %shard_map.46 = f32[64,2048]{1,0:T(8,128)} custom-call(bf16[2048,768]{1,0:T(8,128)(2,1)} %x_hbm.1, bf16[64,2048]{1,0:T(8,128)(2,1)} %bitcast.3, f32[1]{0:T(128)S(6)} %copy.6.length_scale, f32[1]{0:T(128)S(6)} %copy.7.out_scale), custom_call_target="tpu_custom_call" | custom-call | tf_op jit(solution)/shard_map/pallas_call | solution.py:432
  116.0 1.9 %copy.8 = f32[2048,64]{0,1:T(8,128)} copy(f32[2048,64]{0,1:T(8,128)} %bitcast.2) | data formatting | bytes 1048576

commit v9 on v8

--- a/solution.py
+++ b/solution.py
@@ -265,8 +265,8 @@
     arrive_cross(last)
     flush(tiles(1, 1, lambda i, sub: far_tile(0, last, 1), nothing), True)
     to_sib(0, 0).start()
+    to_plus(0, last).start()
     to_plus(0, 0).start()
-    to_plus(0, last).start()
     pend = tiles(1, side // 2, lambda i, sub: own_place(CROSS, last, sub), nothing, False)
     combine(0, 0)
     pend = tiles(1, side // 2, lambda i, sub: own_place(CROSS, last, side // 2 + sub), pend, False)
@@ -300,17 +300,17 @@
     @pl.loop(1, 3)
     def _(k):
         make_y(k)
-        y_plus, y_minus, y_sib, _ = y_copies(k)
-        y_plus.start()
-        y_minus.start()
-        y_sib.start()
+        y_copies(k)[1].start()
+        y_copies(k)[2].start()
         apply_own(k)
 
     first = order(minus, 0)
+    make_y(final)
+    for k in (final, 1, 2):
+        y_copies(k)[0].start()
+    apply_own(final)
     make_y(first)
-    make_y(final)
     y_copies(first)[1].start()
-    y_copies(final)[0].start()
     y_copies(final)[1].start()
     y_copies(first)[0].start()
     y_copies(first)[2].start()
@@ -328,13 +328,10 @@
         y_copies(k)[2].wait_recv()
         apply_nn(1, SIB, OWN, k)
 
-    y_forward(1)
-    y_forward(2)
-
-    @pl.loop(0, 2)
-    def _(i):
-        apply_own(first + i * (final - first))
-
+    apply_own(first)
+
+    for j in (0, 1, 2):
+        y_forward(j)
     spare_cols = pl.ds(mul(spare, T), T)
     for j in range(N_PIECE):
         acc[N_SUM + MINUS, :, pl.ds(mul(order(me, j), T), T)] += dot_nn(
@@ -364,11 +361,15 @@
     y_rest(1)
     y_rest(2)
     far_products(((1, 1), (1, 2)), ((1, 1), (1, 2)))
-    y_forward(0)
+    y_copies(order(me, 0))[3].wait_recv()
+
+    by_row = lambda: far_products(((0, 1), (0, 2)), ())
+    by_col = lambda: far_products((), ((1, 0), (2, 0)))
+    pl.when(swap == 0)(by_col)
+    pl.when(swap != 0)(by_row)
     y_copies(order(me, 0))[1].wait_recv()
-    far_products(((0, 1), (0, 2)), ((1, 0), (2, 0)), (0,))
-    y_copies(order(me, 0))[3].wait_recv()
-    far_products(((0, 1), (0, 2)), ((1, 0), (2, 0)), (1,))
+    pl.when(swap == 0)(by_row)
+    pl.when(swap != 0)(by_col)
     for j in (1, 2):
         to_sib(1, j).start()
         to_plus(1, j).start()

time: 118 us -> 119 us (level)
  no operation moved by 1% of the time
where the time goes in v9:
time: 119 us
  Pallas kernels  116 us (97%)
  local copies, waits for them, and re-layouts  1.87 us (2%)
  between operations  1.31 us (1%)
    pallas_call x1, Pallas kernels, local_program(): pl.pallas_call(functools.partial(kernel, n_row), out_shape=jax.ShapeDtype...  116 us

profile of v9, /device:TPU:112, one launch (start us, length us, event | category | flops | bytes accessed | tf_op | source)
XLA Modules:
  0.0 119.0 jit_solution(18294841734142607994)
XLA Ops:
  1.3 115.8 %shard_map.46 = f32[64,2048]{1,0:T(8,128)} custom-call(bf16[2048,768]{1,0:T(8,128)(2,1)} %x_hbm.1, bf16[64,2048]{1,0:T(8,128)(2,1)} %bitcast.3, f32[1]{0:T(128)S(6)} %copy.6.length_scale, f32[1]{0:T(128)S(6)} %copy.7.out_scale), custom_call_target="tpu_custom_call" | custom-call | tf_op jit(solution)/shard_map/pallas_call | solution.py:433
  117.1 1.9 %copy.8 = f32[2048,64]{0,1:T(8,128)} copy(f32[2048,64]{0,1:T(8,128)} %bitcast.2) | data formatting | bytes 1048576

commit v10 on v8

--- a/solution.py
+++ b/solution.py
@@ -366,16 +366,21 @@
     far_products(((1, 1), (1, 2)), ((1, 1), (1, 2)))
     y_forward(0)
     y_copies(order(me, 0))[1].wait_recv()
-    far_products(((0, 1), (0, 2)), ((1, 0), (2, 0)), (0,))
-    y_copies(order(me, 0))[3].wait_recv()
-    far_products(((0, 1), (0, 2)), ((1, 0), (2, 0)), (1,))
+    by_row = lambda: far_products(((0, 1), (0, 2)), ())
+    by_col = lambda: far_products((), ((1, 0), (2, 0)))
+    pl.when(swap == 0)(by_row)
+    pl.when(swap != 0)(by_col)
     for j in (1, 2):
         to_sib(1, j).start()
+    y_copies(order(me, 0))[3].wait_recv()
+    pl.when(swap == 0)(by_col)
+    pl.when(swap != 0)(by_row)
+    for j in (1, 2):
         to_plus(1, j).start()
+    for j in (1, 2):
+        combine(1, j)
     y_forward(last)
     far_products(((0, 0), (1, 0), (2, 0)), ((0, 0), (0, 1), (0, 2)))
-    for j in (1, 2):
-        combine(1, j)
     y_rest(last)
     far_products(((0, last),), ((0, last),))
     for j in (0, last):

time: 118 us -> 117 us (level)
  no operation moved by 1% of the time
where the time goes in v10:
time: 117 us
  Pallas kernels  114 us (97%)
  local copies, waits for them, and re-layouts  1.87 us (2%)
  between operations  1.31 us (1%)
    pallas_call x1, Pallas kernels, local_program(): pl.pallas_call(functools.partial(kernel, n_row), out_shape=jax.ShapeDtype...  114 us

profile of v10, /device:TPU:112, one launch (start us, length us, event | category | flops | bytes accessed | tf_op | source)
XLA Modules:
  0.0 117.0 jit_solution(2124890768914388591)
XLA Ops:
  1.3 113.8 %shard_map.46 = f32[64,2048]{1,0:T(8,128)} custom-call(bf16[2048,768]{1,0:T(8,128)(2,1)} %x_hbm.1, bf16[64,2048]{1,0:T(8,128)(2,1)} %bitcast.3, f32[1]{0:T(128)S(6)} %copy.6.length_scale, f32[1]{0:T(128)S(6)} %copy.7.out_scale), custom_call_target="tpu_custom_call" | custom-call | tf_op jit(solution)/shard_map/pallas_call | solution.py:437
  115.1 1.9 %copy.8 = f32[2048,64]{0,1:T(8,128)} copy(f32[2048,64]{0,1:T(8,128)} %bitcast.2) | data formatting | bytes 1048576

commit v11 on v10

--- a/solution.py
+++ b/solution.py
@@ -101,7 +101,7 @@
     sib_x.start()
 
     scale = jnp.full((8, 128), length_scale[0], F32)
-    coef_d = (-LOG2E / (scale * scale))[0, 0]
+    coef_d = (-2.0 * LOG2E / (2.0 * scale * scale))[0, 0]
     coef_s = out_scale[0]
     eye = (lax.broadcasted_iota(jnp.int32, (128, 128), 0) == lax.broadcasted_iota(jnp.int32, (128, 128), 1))
 
@@ -366,15 +366,21 @@
     far_products(((1, 1), (1, 2)), ((1, 1), (1, 2)))
     y_forward(0)
     y_copies(order(me, 0))[1].wait_recv()
-    by_row = lambda: far_products(((0, 1), (0, 2)), ())
-    by_col = lambda: far_products((), ((1, 0), (2, 0)))
-    pl.when(swap == 0)(by_row)
-    pl.when(swap != 0)(by_col)
+    def by_row(*pairs):
+        return lambda: far_products(((0, 1), (0, 2)), (), pairs)
+
+    def by_col(*pairs):
+        return lambda: far_products((), ((1, 0), (2, 0)), pairs)
+
+    pl.when(swap == 0)(by_row(1))
+    pl.when(swap != 0)(by_col(1))
     for j in (1, 2):
         to_sib(1, j).start()
+    pl.when(swap == 0)(by_row(0))
+    pl.when(swap != 0)(by_col(0))
     y_copies(order(me, 0))[3].wait_recv()
-    pl.when(swap == 0)(by_col)
-    pl.when(swap != 0)(by_row)
+    pl.when(swap == 0)(by_col(0, 1))
+    pl.when(swap != 0)(by_row(0, 1))
     for j in (1, 2):
         to_plus(1, j).start()
     for j in (1, 2):

time: 117 us -> 117 us (level)
  no operation moved by 1% of the time
where the time goes in v11:
time: 117 us
  Pallas kernels  114 us (97%)
  local copies, waits for them, and re-layouts  1.87 us (2%)
  between operations  1.31 us (1%)
    pallas_call x1, Pallas kernels, local_program(): pl.pallas_call(functools.partial(kernel, n_row), out_shape=jax.ShapeDtype...  114 us

profile of v11, /device:TPU:112, one launch (start us, length us, event | category | flops | bytes accessed | tf_op | source)
XLA Modules:
  0.0 117.0 jit_solution(14704938530818447337)
XLA Ops:
  1.3 113.8 %shard_map.46 = f32[64,2048]{1,0:T(8,128)} custom-call(bf16[2048,768]{1,0:T(8,128)(2,1)} %x_hbm.1, bf16[64,2048]{1,0:T(8,128)(2,1)} %bitcast.3, f32[1]{0:T(128)S(6)} %copy.6.length_scale, f32[1]{0:T(128)S(6)} %copy.7.out_scale), custom_call_target="tpu_custom_call" | custom-call | tf_op jit(solution)/shard_map/pallas_call | solution.py:443
  115.1 1.9 %copy.8 = f32[2048,64]{0,1:T(8,128)} copy(f32[2048,64]{0,1:T(8,128)} %bitcast.2) | data formatting | bytes 1048576

commit v12 on v11

--- a/solution.py
+++ b/solution.py
@@ -218,9 +218,9 @@
         start = mul(order(me, j), T)
         x_recv(0, j).wait_recv()
         forward(j).start()
+        half_norms(MINUS, start, T)
         x_recv(1, j).wait_recv()
         half_norms(PLUS, start, T)
-        half_norms(MINUS, start, T)
 
     def arrive_cross(j):
         forward(j).wait_recv()
@@ -388,9 +388,11 @@
     y_forward(last)
     far_products(((0, 0), (1, 0), (2, 0)), ((0, 0), (0, 1), (0, 2)))
     y_rest(last)
-    far_products(((0, last),), ((0, last),))
+    far_products(((0, last),), ((0, last),), (1,))
     for j in (0, last):
         to_sib(1, j).start()
+    far_products(((0, last),), ((0, last),), (0,))
+    for j in (0, last):
         to_plus(1, j).start()
     apply_nn(0, OWN, OWN, 0)
     apply_sib(0)

time: 117 us -> 117 us (level)
  no operation moved by 1% of the time
where the time goes in v12:
time: 117 us
  Pallas kernels  114 us (97%)
  local copies, waits for them, and re-layouts  1.87 us (2%)
  between operations  1.31 us (1%)
    pallas_call x1, Pallas kernels, local_program(): pl.pallas_call(functools.partial(kernel, n_row), out_shape=jax.ShapeDtype...  114 us

profile of v12, /device:TPU:112, one launch (start us, length us, event | category | flops | bytes accessed | tf_op | source)
XLA Modules:
  0.0 117.0 jit_solution(5727360047223986694)
XLA Ops:
  1.3 113.8 %shard_map.46 = f32[64,2048]{1,0:T(8,128)} custom-call(bf16[2048,768]{1,0:T(8,128)(2,1)} %x_hbm.1, bf16[64,2048]{1,0:T(8,128)(2,1)} %bitcast.3, f32[1]{0:T(128)S(6)} %copy.6.length_scale, f32[1]{0:T(128)S(6)} %copy.7.out_scale), custom_call_target="tpu_custom_call" | custom-call | tf_op jit(solution)/shard_map/pallas_call | solution.py:445
  115.1 1.9 %copy.8 = f32[2048,64]{0,1:T(8,128)} copy(f32[2048,64]{0,1:T(8,128)} %bitcast.2) | data formatting | bytes 1048576
